TPU v7x, 128 devices: a whole 4x4x4 slice. The times are simulated.
128 devices in a mesh: seq: 32 (over y, x, core), head: 4 (over z).
Axes of the slice: x: 4, y: 4, z: 4, core: 2. Of those that a mesh axis runs over, the one named last changes fastest.
Arguments:
- probe_vectors: bfloat16 [8192, 4096], P('seq', 'head'), may hold values from -6 to 6
- source_vectors: bfloat16 [8192, 4096], P('seq', 'head'), may hold values from -6 to 6
- content_vectors: bfloat16 [8192, 4096], P('seq', 'head'), may hold values from -6 to 6
- probe_direction_matrix: bfloat16 [8192, 4096], P('seq', 'head'), may hold values from -6 to 6
- probe_direction_source: bfloat16 [8192, 4096], P('seq', 'head'), may hold values from -6 to 6
- content_direction: bfloat16 [8192, 4096], P('seq', 'head'), may hold values from -6 to 6
- head_table_indices: int32 [32], P('head'), may hold values from 0 to 7
- reset_flags: int32 [8192], P('seq'), may hold values 0 or 1
- projection_matrix: bfloat16 [4096, 4096], P('head'), may hold values from -0.09375 to 0.09375
- regression_goal: bfloat16 [8192, 4096], P('seq'), may hold values from -6 to 6
Outputs:
- hess_q: bfloat16 [8192, 4096], P('seq', 'head')
- hess_k: bfloat16 [8192, 4096], P('seq', 'head')
- hess_v: bfloat16 [8192, 4096], P('seq', 'head')
All inputs are finite; a program needn't handle non-finite values. No bound on the sum of `reset_flags` on one device may be relied on, other than what follows from the above.
Results may differ from a plain program's by a relative error of at most 0.024.
Values may be sent and summed in bfloat16 or wider, within the bound.
A program may use at most 128 MiB of HBM per device.

v0:
```python
import math

import jax
import jax.numpy as jnp
from jax import lax
from jax.sharding import Mesh
from jax.sharding import PartitionSpec as P

LEVELS = 8
SEQ = ("seq_0", "seq_1", "seq_2")


RESET_KEPT_SHARE = 0.7
EPS = 1e-06
HIGHEST = lax.Precision.HIGHEST
PLAIN = lax.Precision.DEFAULT


def filled_with(shard, identity):
    return jax.tree.map(
        lambda part, zero: jnp.zeros_like(part) + jnp.asarray(zero, part.dtype), shard, identity
    )


def carried_in(shard, axes, combine, identity):
    before = start = filled_with(shard, identity)
    subtotal = shard
    for axis in reversed(axes):
        peers, index = (lax.axis_size(axis), lax.axis_index(axis))
        pieces = jax.tree.map(
            lambda part, kind: lax.all_gather(part.astype(kind), axis),
            subtotal,
            (jnp.bfloat16, jnp.bfloat16, jnp.bfloat16),
        )
        inside, subtotal = (start, start)
        for k in range(peers):
            passed = k < index
            subtotal = combine(
                subtotal, jax.tree.map(lambda part, own: part[k].astype(own.dtype), pieces, shard)
            )
            inside = jax.tree.map(lambda new, old: jnp.where(passed, new, old), subtotal, inside)
        before = combine(inside, before)
    return before


def entering(shard, axes, combine, identity):
    before = start = filled_with(shard, identity)
    subtotal = shard
    for axis in reversed(axes):
        peers, index = (lax.axis_size(axis), lax.axis_index(axis))
        pieces = jax.tree.map(
            lambda part, kind: lax.all_gather(part.astype(kind), axis),
            subtotal,
            jax.tree.map(lambda a: jnp.bfloat16 if a.dtype == jnp.float32 else a.dtype, shard),
        )
        inside, subtotal = (start, start)
        for k in reversed(range(peers)):
            passed = k > index
            subtotal = combine(
                subtotal, jax.tree.map(lambda part, own: part[k].astype(own.dtype), pieces, shard)
            )
            inside = jax.tree.map(lambda new, old: jnp.where(passed, new, old), subtotal, inside)
        before = combine(inside, before)
    return before


def log_gammas(head_table_indices, chain_len):
    fraction = head_table_indices.astype(jnp.float32) / (LEVELS - 1)
    rates = jnp.exp(math.log(1.0 / 32.0) + fraction * math.log(16.0 / chain_len))
    return jnp.log1p(-rates)


def segment_rate_exponents(reset_flags, forgetting_exponent):
    running_number = jnp.cumsum(reset_flags).astype(jnp.float32)
    position_indices = jnp.arange(1, reset_flags.shape[0] + 1).astype(jnp.float32)
    return (
        position_indices[:, None] * forgetting_exponent[None, :]
        + math.log(RESET_KEPT_SHARE) * running_number[:, None]
    )


def block_out(q, k, v, state, fading_rate_exponent, score_prec):
    length = q.shape[0]
    scale = q.shape[2] ** (-0.5)
    scores = jnp.einsum("thd,shd->hts", q, k, precision=score_prec) * scale
    later = lax.broadcasted_iota(jnp.int32, (length, length), 0) >= lax.broadcasted_iota(
        jnp.int32, (length, length), 1
    )
    trans = fading_rate_exponent.T
    spread = trans[:, :, None] - trans[:, None, :]
    weights = jnp.where(later[None], jnp.exp(jnp.where(later[None], spread, 0.0)), 0.0)
    inner = jnp.einsum("hts,she->the", scores * weights, v, precision=HIGHEST)
    outer = jnp.exp(fading_rate_exponent)[:, :, None] * jnp.einsum(
        "thd,hde->the", q, state, precision=HIGHEST
    )
    return inner + outer


def block_state(k, v, fading_rate_exponent):
    scale = k.shape[2] ** (-0.5)
    weights = jnp.exp(fading_rate_exponent[-1][None, :] - fading_rate_exponent)
    return jnp.einsum("shd,she->hde", k * (scale * weights[:, :, None]), v, precision=HIGHEST)


def group_norm(outputs):
    return outputs * lax.rsqrt(jnp.mean(outputs * outputs, axis=-1, keepdims=True) + EPS)


def forward_combine(earlier, later):
    factor = later[0][:, None, None]
    return (earlier[0] * later[0], earlier[1] * factor + later[1], earlier[2] * factor + later[2])


def reverse_combine(earlier, later):
    factor = later[0][:, None, None]
    return (earlier[0] * later[0], later[1] + factor * earlier[1], later[2] + factor * earlier[2])


def on_device(
    probe_vectors,
    source_vectors,
    content_vectors,
    probe_direction_matrix,
    probe_direction_source,
    content_direction,
    head_table_indices,
    reset_flags,
    projection_matrix,
    regression_goal,
):
    length = probe_vectors.shape[0]
    heads_here = head_table_indices.shape[0]
    head_width = probe_vectors.shape[1] // heads_here
    chain_len = length * lax.axis_size(SEQ)
    forgetting_exponent = log_gammas(head_table_indices, float(chain_len))
    fading_rate_exponent = segment_rate_exponents(reset_flags, forgetting_exponent)

    def to_heads(array):
        return array.astype(jnp.float32).reshape(length, heads_here, head_width)

    query_rows, key_rows, value_rows = (
        to_heads(probe_vectors),
        to_heads(source_vectors),
        to_heads(content_vectors),
    )
    query_tan, key_tan, value_tan = (
        to_heads(probe_direction_matrix),
        to_heads(probe_direction_source),
        to_heads(content_direction),
    )
    decay_all = jnp.exp(fading_rate_exponent[-1])
    state_own, state_tan = jax.jvp(
        lambda a, b: block_state(a, b, fading_rate_exponent),
        (key_rows, value_rows),
        (key_tan, value_tan),
    )
    ones_decay = jnp.ones_like(decay_all)
    zero_state = jnp.zeros_like(state_own)
    carried = carried_in(
        (decay_all, state_own, state_tan),
        SEQ,
        forward_combine,
        (ones_decay, zero_state, zero_state),
    )
    state_in, state_in_tan = (carried[1], carried[2])
    outputs, outputs_tan = jax.jvp(
        lambda a, b, c, d: block_out(a, b, c, d, fading_rate_exponent, PLAIN),
        (query_rows, key_rows, value_rows, state_in),
        (query_tan, key_tan, value_tan, state_in_tan),
    )
    normed, normed_tan = jax.jvp(group_norm, (outputs,), (outputs_tan,))
    normed_rows = normed.reshape(length, -1).astype(jnp.bfloat16)
    normed_rows_tan = normed_tan.reshape(length, -1).astype(jnp.bfloat16)
    part_sum = jnp.dot(normed_rows, projection_matrix, preferred_element_type=jnp.float32)
    part_sum_tan = jnp.dot(normed_rows_tan, projection_matrix, preferred_element_type=jnp.float32)
    summed, summed_tan = (
        lax.psum(part_sum.astype(jnp.bfloat16), "head").astype(jnp.float32),
        lax.psum(part_sum_tan.astype(jnp.bfloat16), "head").astype(jnp.float32),
    )
    residual = (summed - regression_goal.astype(jnp.float32)).astype(jnp.bfloat16)
    residual_tan = summed_tan.astype(jnp.bfloat16)
    dims = (((1,), (1,)), ((), ()))
    grad_norm = lax.dot_general(
        residual, projection_matrix, dims, preferred_element_type=jnp.float32
    ).reshape(length, heads_here, head_width)
    grad_norm_tan = lax.dot_general(
        residual_tan, projection_matrix, dims, preferred_element_type=jnp.float32
    ).reshape(length, heads_here, head_width)

    def norm_back(point, cotan):
        return jax.vjp(group_norm, point)[1](cotan)[0]

    grad_out, grad_out_tan = jax.jvp(norm_back, (outputs, grad_norm), (outputs_tan, grad_norm_tan))

    def out_grads(a, b, c, d, g):
        return jax.vjp(
            lambda a2, b2, c2, d2: block_out(a2, b2, c2, d2, fading_rate_exponent, HIGHEST),
            a,
            b,
            c,
            d,
        )[1](g)

    primal_g, tangent_g = jax.jvp(
        out_grads,
        (query_rows, key_rows, value_rows, state_in, grad_out),
        (query_tan, key_tan, value_tan, state_in_tan, grad_out_tan),
    )
    returned = entering(
        (decay_all, primal_g[3], tangent_g[3]),
        SEQ,
        reverse_combine,
        (ones_decay, zero_state, zero_state),
    )

    def state_grads(b, c, g):
        return jax.vjp(lambda b2, c2: block_state(b2, c2, fading_rate_exponent), b, c)[1](g)

    extra_tan = jax.jvp(
        state_grads, (key_rows, value_rows, returned[1]), (key_tan, value_tan, returned[2])
    )[1]
    hess_q = tangent_g[0].reshape(length, -1).astype(jnp.bfloat16)
    hess_k = (tangent_g[1] + extra_tan[0]).reshape(length, -1).astype(jnp.bfloat16)
    hess_v = (tangent_g[2] + extra_tan[1]).reshape(length, -1).astype(jnp.bfloat16)
    return (hess_q, hess_k, hess_v)


def solution(mesh):
    split = Mesh(
        mesh.devices.reshape(4, 4, 2, mesh.shape["head"]), ("seq_0", "seq_1", "seq_2", "head")
    )
    return jax.shard_map(
        on_device,
        mesh=split,
        in_specs=(
            P(SEQ, "head"),
            P(SEQ, "head"),
            P(SEQ, "head"),
            P(SEQ, "head"),
            P(SEQ, "head"),
            P(SEQ, "head"),
            P("head"),
            P(SEQ),
            P("head", None),
            P(SEQ, None),
        ),
        out_specs=(P(SEQ, "head"), P(SEQ, "head"), P(SEQ, "head")),
        check_vma=False,
    )
```

profile of v0, /device:TPU:1, one launch (start us, length us, event | category | flops | bytes accessed | tf_op | source)
XLA Modules:
  0.0 397.4 jit_solution(15830459916279035775)
XLA Ops:
  9.8 2.8 all-gather.4
  12.6 7.8 %all-gather.5 = bf16[4,1,8]{2,1,0:T(2,128)(2,1)S(1)} all-gather(bf16[1,1,8]{2,1,0:T(2,128)(2,1)S(1)} %multiply_convert_fusion.1), channel_id=1, replica_groups=mesh['seq_0'=4,'seq_1'=4,'seq_2'=2,'head'=4] {'seq_1'}, dimensions={0}, use_global_device_ids=true | all-gather | bytes 80 | tf_op jit(solution)/shard_map/all_gather | solution.py:31
  25.4 4.2 %all-gather = bf16[16,128,128]{2,1,0:T(8,128)(2,1)S(1)} all-gather(bf16[8,128,128]{2,1,0:T(8,128)(2,1)S(1)} %fusion.31), channel_id=2, replica_groups=mesh['seq_0'=4,'seq_1'=4,'seq_2'=2,'head'=4] {'seq_2'}, dimensions={0}, use_global_device_ids=true | all-gather | bytes 786432 | tf_op jit(solution)/shard_map/all_gather | solution.py:31
  29.5 2.2 all-gather.1
  34.4 8.0 %all-gather.6 = bf16[4,1,8]{2,1,0:T(2,128)(2,1)S(1)} all-gather(bf16[1,1,8]{2,1,0:T(2,128)(2,1)S(1)} %get-tuple-element.46), channel_id=1, replica_groups=mesh['seq_0'=4,'seq_1'=4,'seq_2'=2,'head'=4] {'seq_0'}, dimensions={0}, use_global_device_ids=true | all-gather | bytes 80 | tf_op jit(solution)/shard_map/all_gather | solution.py:31
  44.7 11.0 %all-gather.17.cloned.1.call-done = bf16[4,8,128,128]{3,2,1,0:T(8,128)(2,1)} async-done(((bf16[1,8,128,128]{3,2,1,0:T(8,128)(2,1)}), bf16[4,8,128,128]{3,2,1,0:T(8,128)(2,1)}) %all-gather.17.cloned.1.call-update) | async-done | bytes 1048592 | tf_op jit(solution)/shard_map/all_gather | solution.py:31
  55.7 26.1 %all-gather.21.cloned.1.call-done = bf16[4,8,128,128]{3,2,1,0:T(8,128)(2,1)} async-done(((bf16[1,8,128,128]{3,2,1,0:T(8,128)(2,1)}), bf16[4,8,128,128]{3,2,1,0:T(8,128)(2,1)}) %all-gather.21.cloned.1.call-update) | async-done | bytes 1048592 | tf_op jit(solution)/shard_map/all_gather | solution.py:31
  81.8 2.9 fusion.103
  84.8 1.8 fusion.191
  88.7 2.3 convolution_bitcast_fusion
  92.8 2.0 fusion.8
  94.8 2.4 fusion.24
  97.2 12.1 %all-gather.19.cloned.1.call-done = bf16[4,8,128,128]{3,2,1,0:T(8,128)(2,1)} async-done(((bf16[1,8,128,128]{3,2,1,0:T(8,128)(2,1)}), bf16[4,8,128,128]{3,2,1,0:T(8,128)(2,1)}) %all-gather.19.cloned.1.call-update) | async-done | bytes 1048592 | tf_op jit(solution)/shard_map/all_gather | solution.py:31
  109.3 2.6 fusion.89
  113.5 21.8 %all-gather.23.cloned.1.call-done = bf16[4,8,128,128]{3,2,1,0:T(8,128)(2,1)} async-done(((bf16[1,8,128,128]{3,2,1,0:T(8,128)(2,1)}), bf16[4,8,128,128]{3,2,1,0:T(8,128)(2,1)}) %all-gather.23.cloned.1.call-update) | async-done | bytes 1048592 | tf_op jit(solution)/shard_map/all_gather | solution.py:31
  135.3 2.7 fusion.86
  140.6 7.6 %convolution_convert_fusion = bf16[256,4096]{1,0:T(8,128)(2,1)} fusion(bf16[256,1024]{0,1:T(8,128)(2,1)S(1)} %bitcast.690, bf16[1024,4096]{1,0:T(8,128)(2,1)} %param.18), kind=kOutput, calls=%fused_computation | convolution fusion | flops 2148532224 | bytes 11010048 | tf_op jit(solution)/shard_map/dot_general | solution.py:174
  148.2 4.2 %convolution_convert_fusion.1 = bf16[256,4096]{1,0:T(8,128)(2,1)} fusion(bf16[256,1024]{0,1:T(8,128)(2,1)S(1)} %bitcast.689, bf16[1024,4096]{1,0:T(8,128)(2,1)S(1)} %bitcast.673), kind=kOutput, calls=%fused_computation.1 | convolution fusion | flops 2148532224 | bytes 11010048 | tf_op jit(solution)/shard_map/dot_general | solution.py:175
  152.5 95.4 %all-reduce.3.cloned.1.call-done = (bf16[256,4096]{1,0:T(8,128)(2,1)}, bf16[256,4096]{1,0:T(8,128)(2,1)}) async-done(((bf16[256,4096]{1,0:T(8,128)(2,1)}, bf16[256,4096]{1,0:T(8,128)(2,1)}), (bf16[256,4096]{1,0:T(8,128)(2,1)}, bf16[256,4096]{1,0:T(8,128)(2,1)})) %all-reduce.3.cloned.1.call-update) | async-done | bytes 4194320 | tf_op jit(solution)/shard_map/psum | solution.py:177
  247.9 6.5 %fusion.289 = f32[256,1024]{0,1:T(8,128)S(1)} fusion(bf16[256,4096]{1,0:T(8,128)(2,1)} %get-tuple-element.23, bf16[1024,4096]{1,0:T(8,128)(2,1)} %param.18), kind=kOutput, calls=%fused_computation.443 | convolution fusion | flops 2147483648 | bytes 11534336 | tf_op jit(solution)/shard_map/dot_general | solution.py:186
  254.5 5.9 %add_reduce_fusion = (f32[256,8]{0,1:T(8,128)S(1)}, f32[256,8]{0,1:T(8,128)S(1)}, f32[256,1024]{0,1:T(8,128)S(1)}) fusion(f32[256,8,128]{0,2,1:T(8,128)S(1)} %get-tuple-element.64, f32[256,8,128]{0,2,1:T(8,128)S(1)} %fusion.22, f32[256,1024]{0,1:T(8,128)S(1)} %fusion.289, bf16[1024,4096]{1,0:T(8,128)(2,1)} %param.18, bf16[256,4096]{1,0:T(8,128)(2,1)S(1)} %copy-done.44, ...), kind=kOutput, calls=%fused_computation.68 | convolution fusion | flops 2153246720 | bytes 16793600 | tf_op jit(solution)/shard_map/dot_general | solution.py:183
  260.5 2.2 add_add_fusion
  265.4 1.8 copy.233
  267.2 5.8 %all-gather.2 = bf16[16,128,128]{2,1,0:T(8,128)(2,1)} all-gather(bf16[8,128,128]{2,1,0:T(8,128)(2,1)} %copy.233), channel_id=4, replica_groups=mesh['seq_0'=4,'seq_1'=4,'seq_2'=2,'head'=4] {'seq_2'}, dimensions={0}, use_global_device_ids=true | all-gather | bytes 786432 | tf_op jit(solution)/shard_map/all_gather | solution.py:52
  273.8 2.4 all-gather.3
  277.0 2.1 fusion.161
  279.2 7.8 %all-gather.7 = bf16[4,1,8]{2,1,0:T(2,128)(2,1)S(1)} all-gather(bf16[1,1,8]{2,1,0:T(2,128)(2,1)S(1)} %get-tuple-element.45), channel_id=1, replica_groups=mesh['seq_0'=4,'seq_1'=4,'seq_2'=2,'head'=4] {'seq_0'}, dimensions={0}, use_global_device_ids=true | all-gather | bytes 80 | tf_op jit(solution)/shard_map/all_gather | solution.py:52
  287.0 2.8 fusion.171
  289.9 1.8 fusion.183
  291.8 1.8 fusion.185
  294.6 1.8 multiply_multiply_fusion.1
  297.7 2.3 fusion.290
  300.5 26.7 %all-gather.29.cloned.1.call-done = bf16[4,8,128,128]{3,2,1,0:T(8,128)(2,1)} async-done(((bf16[1,8,128,128]{3,2,1,0:T(8,128)(2,1)}), bf16[4,8,128,128]{3,2,1,0:T(8,128)(2,1)}) %all-gather.29.cloned.1.call-update) | async-done | bytes 1048592 | tf_op jit(solution)/shard_map/all_gather | solution.py:52
  327.2 2.9 fusion.137
  330.3 2.2 fusion.46
  335.7 2.0 fusion.28
  337.9 3.0 fusion.1
  341.0 3.7 fusion.181
  345.7 4.0 %fusion.23 = f32[256,8,128]{0,2,1:T(8,128)} fusion(f32[8,256,128]{1,2,0:T(8,128)} %fusion.181, f32[8,256,256]{2,1,0:T(8,128)} %copy-done.22, bf16[256,1024]{1,0:T(8,128)(2,1)S(1)} %copy-done.9), kind=kOutput, calls=%fused_computation.38 | convolution fusion | flops 805568512 | bytes 4718592 | tf_op jit(solution)/shard_map/jvp(transpose(jvp(thd,shd->hts)))/dot_general | solution.py:85
  349.7 3.0 fusion.25
  352.8 1.9 all-gather.27.cloned.1.call-done
  354.7 2.9 fusion.83
  359.2 2.1 fusion.48
  361.3 19.6 %all-gather.31.cloned.1.call-done = bf16[4,8,128,128]{3,2,1,0:T(8,128)(2,1)} async-done(((bf16[1,8,128,128]{3,2,1,0:T(8,128)(2,1)}), bf16[4,8,128,128]{3,2,1,0:T(8,128)(2,1)}) %all-gather.31.cloned.1.call-update) | async-done | bytes 1048592 | tf_op jit(solution)/shard_map/all_gather | solution.py:52
  380.9 2.8 fusion.80
  383.8 2.0 fusion.30
  385.7 2.0 copy.250
  387.8 1.8 fusion.29
  (165 shorter events, 35.3 us)
Async XLA Ops:
  7.2 77.7 %copy-start = (bf16[256,1024]{1,0:T(8,128)(2,1)S(1)}, bf16[256,1024]{1,0:T(8,128)(2,1)}, u32[]{:S(2)}) copy-start(bf16[256,1024]{1,0:T(8,128)(2,1)} %param.10) | copy-start | bytes 1572868
  7.2 16.0 %copy-start.18 = (bf16[256,1024]{1,0:T(8,128)(2,1)S(1)}, bf16[256,1024]{1,0:T(8,128)(2,1)}, u32[]{:S(2)}) copy-start(bf16[256,1024]{1,0:T(8,128)(2,1)} %param.12) | copy-start | bytes 1572868
  7.2 48.5 %all-gather.17.cloned.1.call-start = ((), (), s32[]{:S(2)}) async-start(), calls=%async_computation | async-start | bytes 1310720 | tf_op jit(solution)/shard_map/all_gather | solution.py:31
  21.7 63.1 %copy-start.1 = (bf16[256,1024]{0,1:T(8,128)(2,1)}, bf16[256,1024]{0,1:T(8,128)(2,1)S(1)}, u32[]{:S(2)}) copy-start(bf16[256,1024]{0,1:T(8,128)(2,1)S(1)} %copy.207) | copy-start | bytes 1572868
  21.8 2.9 copy-start.11
  29.5 4.1 %copy-start.30 = (bf16[16,128,128]{2,1,0:T(8,128)(2,1)}, bf16[16,128,128]{2,1,0:T(8,128)(2,1)S(1)}, u32[]{:S(2)}) copy-start(bf16[16,128,128]{2,1,0:T(8,128)(2,1)S(1)} %all-gather) | copy-start | bytes 1572868
  33.6 48.2 %all-gather.21.cloned.1.call-start = ((), (), s32[]{:S(2)}) async-start(), calls=%async_computation.2 | async-start | bytes 1310720 | tf_op jit(solution)/shard_map/all_gather | solution.py:31
  34.4 74.9 %all-gather.19.cloned.1.call-start = ((), (), s32[]{:S(2)}) async-start(), calls=%async_computation.1 | async-start | bytes 1310720 | tf_op jit(solution)/shard_map/all_gather | solution.py:31
  84.7 50.6 %all-gather.23.cloned.1.call-start = ((), (), s32[]{:S(2)}) async-start(), calls=%async_computation.3 | async-start | bytes 1310720 | tf_op jit(solution)/shard_map/all_gather | solution.py:31
  88.7 2.6 copy-start.7
  91.0 156.9 %all-reduce.3.cloned.1.call-start = ((), (), s32[]{:S(2)}) async-start(), calls=%async_computation.8 | async-start | bytes 8388608 | tf_op jit(solution)/shard_map/psum | solution.py:177
  91.3 1.6 copy-start.24
  92.8 2.0 copy-start.17
  94.8 14.5 %copy-start.31 = (bf16[16,128,128]{2,1,0:T(8,128)(2,1)S(1)}, bf16[16,128,128]{2,1,0:T(8,128)(2,1)}, u32[]{:S(2)}) copy-start(bf16[16,128,128]{2,1,0:T(8,128)(2,1)} %copy-done.30) | copy-start | bytes 1572868
  109.3 26.0 %copy-start.29 = (bf16[16,128,128]{2,1,0:T(8,128)(2,1)S(1)}, bf16[16,128,128]{2,1,0:T(8,128)(2,1)}, u32[]{:S(2)}) copy-start(bf16[16,128,128]{2,1,0:T(8,128)(2,1)} %copy-done.28) | copy-start | bytes 1572868
  111.9 26.1 %copy-start.33 = (f32[8,128,128]{2,1,0:T(8,128)}, f32[8,128,128]{2,1,0:T(8,128)S(1)}, u32[]{:S(2)}) copy-start(f32[8,128,128]{2,1,0:T(8,128)S(1)} %fusion.89) | copy-start | bytes 1572868
  135.3 2.7 copy-start.41
  135.3 2.7 copy-start.42
  139.4 115.1 %copy-start.6 = (f32[256,8,128]{0,2,1:T(8,128)}, f32[256,8,128]{0,2,1:T(8,128)S(1)}, u32[]{:S(2)}) copy-start(f32[256,8,128]{0,2,1:T(8,128)S(1)} %fusion.22) | copy-start | bytes 3145732
  140.3 114.2 %copy-start.10 = (f32[256,8,128]{0,2,1:T(8,128)}, f32[256,8,128]{0,2,1:T(8,128)S(1)}, u32[]{:S(2)}) copy-start(f32[256,8,128]{0,2,1:T(8,128)S(1)} %get-tuple-element.64) | copy-start | bytes 3145732
  140.3 7.9 %slice-start = ((s8[8388608]{0:T(1024)(128)(4,1)}), s8[4194304]{0:T(1024)(128)(4,1)S(1)}, s32[]{:S(2)}) async-start(s8[8388608]{0:T(1024)(128)(4,1)} %bitcast.672), calls=%async_computation.9 | async-start | bytes 8388608
  140.6 7.6 %slice-start.1 = ((s8[8388608]{0:T(1024)(128)(4,1)}), s8[4194304]{0:T(1024)(128)(4,1)S(1)}, s32[]{:S(2)}) async-start(s8[8388608]{0:T(1024)(128)(4,1)} %bitcast.672), calls=%async_computation.10 | async-start | bytes 8388608
  152.5 148.0 %all-gather.25.cloned.1.call-start = ((), (), s32[]{:S(2)}) async-start(), calls=%async_computation.4 | async-start | bytes 1310720 | tf_op jit(solution)/shard_map/all_gather | solution.py:52
  247.9 6.6 %copy-start.44 = (bf16[256,4096]{1,0:T(8,128)(2,1)S(1)}, bf16[256,4096]{1,0:T(8,128)(2,1)}, u32[]{:S(2)}) copy-start(bf16[256,4096]{1,0:T(8,128)(2,1)} %param.19) | copy-start | bytes 6291460
  247.9 6.6 %copy-start.45 = (bf16[256,4096]{1,0:T(8,128)(2,1)S(1)}, bf16[256,4096]{1,0:T(8,128)(2,1)}, u32[]{:S(2)}) copy-start(bf16[256,4096]{1,0:T(8,128)(2,1)} %get-tuple-element.22) | copy-start | bytes 6291460
  279.2 48.0 %all-gather.29.cloned.1.call-start = ((), (), s32[]{:S(2)}) async-start(), calls=%async_computation.6 | async-start | bytes 1310720 | tf_op jit(solution)/shard_map/all_gather | solution.py:52
  279.2 10.7 %copy-start.2 = (bf16[256,1024]{0,1:T(8,128)(2,1)S(1)}, bf16[256,1024]{0,1:T(8,128)(2,1)}, u32[]{:S(2)}) copy-start(bf16[256,1024]{0,1:T(8,128)(2,1)} %copy-done.1) | copy-start | bytes 1572868
  291.7 63.0 %all-gather.27.cloned.1.call-start = ((), (), s32[]{:S(2)}) async-start(), calls=%async_computation.5 | async-start | bytes 1310720 | tf_op jit(solution)/shard_map/all_gather | solution.py:52
  291.8 1.8 copy-start.19
  330.1 50.8 %all-gather.31.cloned.1.call-start = ((), (), s32[]{:S(2)}) async-start(), calls=%async_computation.7 | async-start | bytes 1310720 | tf_op jit(solution)/shard_map/all_gather | solution.py:52
  330.3 2.2 copy-start.20
  332.5 1.7 copy-start.3
  332.5 1.7 copy-start.39
  334.2 1.4 copy-start.34
  335.7 2.0 copy-start.14
  335.7 2.2 copy-start.15
  340.9 3.8 copy-start.43
  341.0 4.8 %copy-start.9 = (bf16[256,1024]{1,0:T(8,128)(2,1)S(1)}, bf16[256,1024]{1,0:T(8,128)(2,1)}, u32[]{:S(2)}) copy-start(bf16[256,1024]{1,0:T(8,128)(2,1)} %param.13) | copy-start | bytes 1572868
  345.7 4.0 %copy-start.23 = (f32[8,256,256]{2,1,0:T(8,128)S(1)}, f32[8,256,256]{2,1,0:T(8,128)}, u32[]{:S(2)}) copy-start(f32[8,256,256]{2,1,0:T(8,128)} %fusion.185) | copy-start | bytes 6291460
  345.7 4.0 %copy-start.40 = (f32[8,128,256]{2,1,0:T(8,128)S(1)}, f32[8,128,256]{2,1,0:T(8,128)}, u32[]{:S(2)}) copy-start(f32[8,128,256]{2,1,0:T(8,128)} %fusion.1) | copy-start | bytes 3145732
  349.7 5.0 %copy-start.32 = (bf16[16,128,128]{2,1,0:T(8,128)(2,1)S(1)}, bf16[16,128,128]{2,1,0:T(8,128)(2,1)}, u32[]{:S(2)}) copy-start(bf16[16,128,128]{2,1,0:T(8,128)(2,1)} %all-gather.2) | copy-start | bytes 1572868
  352.8 4.9 %copy-start.21 = (bf16[256,1024]{1,0:T(8,128)(2,1)S(1)}, bf16[256,1024]{1,0:T(8,128)(2,1)}, u32[]{:S(2)}) copy-start(bf16[256,1024]{1,0:T(8,128)(2,1)} %param.12) | copy-start | bytes 1572868
  357.6 23.2 %copy-start.27 = (bf16[16,128,128]{2,1,0:T(8,128)(2,1)S(1)}, bf16[16,128,128]{2,1,0:T(8,128)(2,1)}, u32[]{:S(2)}) copy-start(bf16[16,128,128]{2,1,0:T(8,128)(2,1)} %copy-done.26) | copy-start | bytes 1572868
  361.3 22.4 %copy-start.4 = (bf16[256,1024]{0,1:T(8,128)(2,1)S(1)}, bf16[256,1024]{0,1:T(8,128)(2,1)}, u32[]{:S(2)}) copy-start(bf16[256,1024]{0,1:T(8,128)(2,1)} %copy-done.1) | copy-start | bytes 1572868
  380.9 2.9 copy-start.36
  380.9 2.9 copy-start.38
  383.7 4.0 %copy-start.13 = (bf16[256,1024]{1,0:T(8,128)(2,1)S(1)}, bf16[256,1024]{1,0:T(8,128)(2,1)}, u32[]{:S(2)}) copy-start(bf16[256,1024]{1,0:T(8,128)(2,1)} %param.15) | copy-start | bytes 1572868
  383.8 4.0 %copy-start.35 = (f32[8,128,256]{2,1,0:T(8,128)S(1)}, f32[8,128,256]{2,1,0:T(8,128)}, u32[]{:S(2)}) copy-start(f32[8,128,256]{2,1,0:T(8,128)} %fusion.164) | copy-start | bytes 3145732
  (9 other events, 10.4 us)
Sparse Core Ops, SparseCore 0:
  33.7 21.8 all-gather.16
  57.3 24.4 all-gather.20
  84.8 24.4 all-gather.18
  110.8 24.4 all-gather.22
  152.6 95.3 all-reduce.2
  279.3 21.1 all-gather.24
  302.7 24.4 all-gather.28
  330.2 24.4 all-gather.26
  356.4 24.4 all-gather.30
where the time goes:
time: 405 us; the launch traced here: 397 us
  waiting for transfers between devices  216 us (53%)
  matrix products  81.9 us (20%)
  blocking collectives  40.9 us (10%)
  other arithmetic  24.7 us (6%)
  local copies, waits for them, and re-layouts  18.5 us (5%)
  between operations  14.8 us (4%)
    psum x1, waiting for transfers between devices, on_device(): lax.psum(part_sum.astype(jnp.bfloat16), 'head').astype(jnp.float32)  95.4 us
    all_gather x4, waiting for transfers between devices, carried_in(): lax.all_gather(part.astype(kind), axis)  71 us
    all_gather x4, waiting for transfers between devices, entering(): lax.all_gather(part.astype(kind), axis)  48.7 us
    all_gather x5, blocking collectives, carried_in(): lax.all_gather(part.astype(kind), axis)  25 us
    dot_general x10, matrix products, block_out(): scores = jnp.einsum('thd,shd->hts', q, k, precision=score_prec) * scale  20.7 us
    dot_general x8, matrix products, block_out(): inner = jnp.einsum('hts,she->the', scores * weights, v, precision=HIGHEST)  17.2 us
    all_gather x3, blocking collectives, entering(): lax.all_gather(part.astype(kind), axis)  16 us
    unnamed x102, local copies, waits for them, and re-layouts  14.1 us
  transfers between devices with their start and end apart: 9, of which 9 were waited for; matrix products, arithmetic and copies ran while one was open for 14% of the time, Pallas kernels for 0%

commit v1 on v0

v1 whole, which is shorter than its diff:
```python
import functools
import math

import jax
import jax.numpy as jnp
from jax import lax
from jax.experimental import pallas as pl
from jax.experimental.pallas import tpu as pltpu
from jax.sharding import PartitionSpec as P

LEVELS = 8
KEPT_LOG = math.log(0.7)
EPS = 1e-06
F32 = jnp.float32
BF16 = jnp.bfloat16
MESH = pl.DeviceIdType.MESH
FAR = 1e9


def dot(a, b, dims=((1,), (0,))):
    return lax.dot_general(a, b, (dims, ((), ())), preferred_element_type=F32)


def cols(h, d):
    return pl.ds(pl.multiple_of(h * d, d), d)


def decay_tables(flags_ref, dist, fall, pos, cum):
    t = dist.shape[0]
    row = lax.broadcasted_iota(jnp.int32, (t, t), 0)
    col = lax.broadcasted_iota(jnp.int32, (t, t), 1)
    flags = jnp.broadcast_to(flags_ref[...].astype(F32), (t, t))
    cum_col = jnp.sum(jnp.where(col <= row, flags, 0.0), axis=1, keepdims=True)
    flag_col = jnp.sum(jnp.where(col == row, flags, 0.0), axis=1, keepdims=True)
    cum_row = jnp.sum(jnp.where(row <= col, flag_col, 0.0), axis=0, keepdims=True)
    dist[...] = jnp.where(row >= col, (row - col).astype(F32), FAR)
    fall[...] = KEPT_LOG * (cum_col - cum_row)
    pos[...] = lax.broadcasted_iota(jnp.int32, pos.shape, 0).astype(F32)
    cum[...] = KEPT_LOG * jnp.broadcast_to(cum_col, cum.shape)


def barrier_start(n, me, up, down):
    barrier = pltpu.get_barrier_semaphore()
    for z in (up, down):
        pl.semaphore_signal(barrier, inc=1, device_id={"head": z}, device_id_type=MESH)

    @pl.loop(1, n)
    def _(step):
        pl.semaphore_signal(barrier, inc=1, device_id={"seq": lax.rem(me + step, n)}, device_id_type=MESH)


def barrier_end(n):
    pl.semaphore_wait(pltpu.get_barrier_semaphore(), n + 1)


def exchange_start(n, me, src, dst, send_sem, recv_sem):
    @pl.loop(1, n)
    def _(step):
        j = lax.rem(me + step, n)
        pltpu.make_async_remote_copy(
            src_ref=src.at[j], dst_ref=dst.at[me], send_sem=send_sem.at[j], recv_sem=recv_sem.at[me],
            device_id={"seq": j}, device_id_type=MESH,
        ).start()


def exchange_end(n, me, src, dst, send_sem, recv_sem):
    @pl.loop(1, n)
    def _(step):
        j = lax.rem(me + step, n)
        pltpu.make_async_remote_copy(
            src_ref=src.at[j], dst_ref=dst.at[j], send_sem=send_sem.at[j], recv_sem=recv_sem.at[j],
            device_id={"seq": j}, device_id_type=MESH,
        ).wait()


def scan_slots(n, me, length, heads, lg_ref, count_ref, own, recv, back, result, reverse):
    recv[me] = own[me]
    head = me // (n // heads)
    lg = lg_ref[head, :, 0:128]

    def step(i, run):
        j = n - 1 - i if reverse else i
        back[j] = run.astype(BF16)
        factor = jnp.exp(float(length) * lg + KEPT_LOG * count_ref[j])
        return run * factor + recv[j].astype(F32)

    lax.fori_loop(0, n, step, jnp.zeros(recv.shape[1:], F32))
    result[me] = back[me]


def state_of(result, h, per, half):
    rows = result.shape[1] // 2
    part = result[pl.ds(h * per, per), half * rows:(half + 1) * rows, :]
    return part.reshape(per * rows, part.shape[2])


def put_state(own, h, per, half, value):
    rows = own.shape[1] // 2
    own[pl.ds(h * per, per), half * rows:(half + 1) * rows, :] = value.astype(BF16).reshape(per, rows, value.shape[1])


def weights_of(h, d, lg_ref, dist, fall):
    return jnp.exp(dist[...] * lg_ref[h] + fall[...]) * (d ** -0.5)


def remote(src, dst, send_sem, recv_sem, **where):
    return pltpu.make_async_remote_copy(
        src_ref=src, dst_ref=dst, send_sem=send_sem, recv_sem=recv_sem, device_id=where, device_id_type=MESH
    )


def arrival(dst, recv_sem):
    pltpu.make_async_copy(dst, dst, recv_sem).wait()


class GramGather:
    def __init__(self, me, full, send_sem, recv_sem):
        c = lax.rem(me, 2)
        x, y = lax.rem(me // 2, 4), me // 8
        self.me, self.c, self.f, self.s = me, c, x + c * (y - x), y + c * (x - y)
        self.full, self.send_sem, self.recv_sem = full, send_sem, recv_sem
        self.rows = full.shape[1] // 32
        self.started = []

    def at(self, df, s_off, absolute=False):
        f = df if absolute else lax.rem(self.f + df + 4, 4)
        s = lax.rem(self.s + s_off + 4, 4)
        return (f * (1 + 3 * self.c) + s * (4 - 3 * self.c)) * 2 + self.c

    def view(self, piece, half=None):
        rows = pl.ds(pl.multiple_of(piece * self.rows, self.rows), self.rows)
        if half is None:
            return self.full.at[:, rows, :]
        return self.full.at[2 * half:2 * half + 2, rows, :]

    def send(self, piece, to, half=None):
        copy = remote(
            self.view(piece, half), self.view(piece, half),
            self.send_sem.at[len(self.started)], self.recv_sem.at[piece, half or 0], seq=to,
        )
        copy.start()
        self.started.append(copy)

    def wait(self, piece, half=None):
        arrival(self.view(piece, half), self.recv_sem.at[piece, half or 0])

    def spread(self, piece):
        self.send(piece, self.at(0, 1))
        self.send(piece, self.at(0, -1))
        self.send(piece, self.me + 1 - 2 * self.c)

    def round(self, k):
        if k == 0:
            self.send(self.me, self.at(1, 0))
            self.send(self.me, self.at(-1, 0))
            self.spread(self.me)
        elif k == 1:
            for step, half in ((-1, 0), (1, 1)):
                piece = self.at(step, 0)
                self.wait(piece)
                self.send(piece, self.at(-step, 0), half)
                self.spread(piece)
        elif k == 2:
            piece = self.at(2, 0)
            self.wait(piece, 0)
            self.wait(piece, 1)
            self.spread(piece)
        elif k == 3:
            for df in (0, -1, 1, 2):
                for step, half in ((-1, 0), (1, 1)):
                    piece = self.at(df, step)
                    self.wait(piece)
                    self.send(piece, self.at(0, -step), half)
                    self.send(piece, self.me + 1 - 2 * self.c)
        elif k == 4:
            for df in (0, -1, 1, 2):
                piece = self.at(df, 2)
                self.wait(piece, 0)
                self.wait(piece, 1)
                self.send(piece, self.me + 1 - 2 * self.c)
        else:

            @pl.loop(0, 16)
            def _(i):
                self.wait(2 * i + 1 - self.c)

    def finish(self):
        for copy in self.started:
            copy.wait_send()


def kernel(
    n, heads, groups, *refs,
):
    inputs, (lg, flags, w_hbm, goal_hbm), (hq, hk, hv) = refs[:6], refs[6:10], refs[10:13]
    (q, k, v, qt, kt, vt, weight, goal, dist, fall, pos, cum, mine, count, own, recv, back, state, own_b, recv_b, back_b,
     state_b, picked, gram, zall, gz, o_buf, ot_buf, g_buf, gt_buf, hk_buf, hv_buf,
     load_sem, s1, r1, s2, r2, s3, r3, s4, r4, s5, r5, ws, wr, gs, gr, zs, zr) = refs[13:]
    me, z = lax.axis_index("seq"), lax.axis_index("head")
    up, down = lax.rem(z + 1, groups), lax.rem(z + groups - 1, groups)
    far = lax.rem(z + 2, groups)
    length, width = q.shape
    d = width // heads
    per = n // heads
    scale = d ** -0.5
    loads = [
        pltpu.make_async_copy(src, dst, load_sem.at[i])
        for i, (src, dst) in enumerate(
            zip((*inputs, w_hbm, goal_hbm), (q, k, v, qt, kt, vt, weight, goal))
        )
    ]
    for i in (1, 2, 4, 5, 6, 0, 3, 7):
        loads[i].start()
    barrier_start(n, me, up, down)
    decay_tables(flags, dist, fall, pos, cum)
    total = jnp.broadcast_to(jnp.sum(flags[...].astype(F32), axis=1, keepdims=True), (1, 128))
    mine[0] = total
    count[me] = total
    for i in (1, 2, 4, 5):
        loads[i].wait()

    @pl.loop(0, heads)
    def _(h):
        c = cols(h, d)
        w = scale * jnp.exp((length - 1.0 - pos[...]) * lg[h, :, 0:d] + (KEPT_LOG * total - cum[...]))
        kw = (k[:, c].astype(F32) * w).astype(BF16)
        ktw = (kt[:, c].astype(F32) * w).astype(BF16)
        both = dot(kw, jnp.concatenate([v[:, c], vt[:, c]], axis=1), ((0,), (0,)))
        put_state(own, h, per, 0, both[:, :d])
        put_state(own, h, per, 1, both[:, d:] + dot(ktw, v[:, c], ((0,), (0,))))

    loads[6].wait()
    barrier_end(n)
    rows = width // n
    half = rows // 2
    mine_rows = pl.ds(pl.multiple_of(me * rows, rows), rows)
    w_copies = [
        remote(weight.at[mine_rows], picked.at[z], ws.at[0], wr.at[0], head=up),
        remote(weight.at[mine_rows], picked.at[z], ws.at[1], wr.at[1], head=down),
    ]
    for copy in w_copies:
        copy.start()

    @pl.loop(1, n)
    def _(step):
        j = lax.rem(me + step, n)
        remote(mine.at[0], count.at[me], s3.at[j], r3.at[me], seq=j).start()

    exchange_start(n, me, own, recv, s1, r1)
    loads[0].wait()
    loads[3].wait()

    def inner(h):
        c = cols(h, d)
        w = weights_of(h, d, lg, dist, fall)
        a = dot(q[:, c], k[:, c], ((1,), (1,)))
        at = dot(
            jnp.concatenate([qt[:, c], q[:, c]], axis=1), jnp.concatenate([k[:, c], kt[:, c]], axis=1), ((1,), (1,))
        )
        p = (a * w).astype(BF16)
        pt = (at * w).astype(BF16)
        both = dot(p, jnp.concatenate([v[:, c], vt[:, c]], axis=1))
        o_buf[:, c] = both[:, :d]
        ot_buf[:, c] = both[:, d:] + dot(pt, v[:, c])

    pl.loop(0, heads // 2)(inner)
    picked[z] = weight[mine_rows]
    arrival(picked.at[down], wr.at[0])
    w_copies.append(remote(picked.at[down, 0:half], picked.at[down, 0:half], ws.at[2], wr.at[2], head=up))
    w_copies[2].start()
    arrival(picked.at[up], wr.at[1])
    w_copies.append(remote(picked.at[up, half:rows], picked.at[up, half:rows], ws.at[3], wr.at[3], head=down))
    w_copies[3].start()

    @pl.loop(1, n)
    def _(step):
        j = lax.rem(me + step, n)
        remote(mine.at[0], count.at[j], s3.at[j], r3.at[j], seq=j).wait()

    exchange_end(n, me, own, recv, s1, r1)
    scan_slots(n, me, length, heads, lg, count, own, recv, back, state, False)
    exchange_start(n, me, back, state, s2, r2)
    arrival(picked.at[far, 0:half], wr.at[2])
    arrival(picked.at[far, half:rows], wr.at[3])
    tile = 256

    @pl.loop(0, width // tile)
    def _(i):
        c = cols(i, tile)
        part = dot(picked[...].reshape(groups * rows, weight.shape[1]), weight[c, :], ((1,), (1,)))
        gram[:, mine_rows, c] = part.astype(BF16).reshape(groups, rows, tile)

    pl.loop(heads // 2, heads)(inner)
    gather = GramGather(me, gram, gs, gr)
    gather.round(0)
    exchange_end(n, me, back, state, s2, r2)

    def z_send(h):
        c = cols(h, d)
        remote(zall.at[z, :, c], zall.at[z, :, c], zs.at[h, 0], zr.at[h, 0], head=up).start()
        remote(zall.at[z, :, c], zall.at[z, :, c], zs.at[h, 1], zr.at[h, 1], head=down).start()

    @pl.loop(0, heads)
    def _(h):
        c = cols(h, d)
        dq = jnp.exp((pos[...] + 1.0) * lg[h, :, 0:d] + cum[...])
        s = state_of(state, h, per, 0)
        st = state_of(state, h, per, 1)
        both = dot(q[:, c], jnp.concatenate([s, st], axis=1))
        o = o_buf[:, c] + dq * both[:, :d]
        ot = ot_buf[:, c] + dq * (both[:, d:] + dot(qt[:, c], s))
        o_buf[:, c] = o
        ot_buf[:, c] = ot
        r = lax.rsqrt(jnp.mean(o * o, axis=1, keepdims=True) + EPS)
        m = jnp.mean(o * ot, axis=1, keepdims=True)
        zall[z, 0:length, c] = (o * r).astype(BF16)
        zall[z, length:, c] = (r * ot - o * (r * r * r * m)).astype(BF16)

        @pl.when(h > 0)
        def _():
            z_send(h - 1)

    loads[7].wait()
    z_send(heads - 1)

    def relay(h):
        c = slice(h * d, (h + 1) * d)
        arrival(zall.at[down, :, c], zr.at[h, 0])
        remote(zall.at[down, 0:length, c], zall.at[down, 0:length, c], zs.at[h, 2], zr.at[h, 2], head=up).start()
        arrival(zall.at[up, :, c], zr.at[h, 1])
        remote(zall.at[up, length:, c], zall.at[up, length:, c], zs.at[h, 3], zr.at[h, 3], head=down).start()

    def distant(h):
        c = slice(h * d, (h + 1) * d)
        arrival(zall.at[far, 0:length, c], zr.at[h, 2])
        arrival(zall.at[far, length:, c], zr.at[h, 3])

    def add(p, *sources):
        part = slice(2 * p * d, 2 * (p + 1) * d)

        @pl.loop(0, width // tile)
        def _(i):
            c = cols(i, tile)
            value = gz[:, c]
            for g in sources:
                value = value + dot(zall[g, :, part], gram[g, part, c])
            gz[:, c] = value

    gather.round(1)
    relay(0)
    gather.round(2)
    relay(1)
    gather.round(3)
    relay(2)
    gather.round(4)
    relay(3)
    gz[length:, :] = jnp.zeros((length, width), F32)

    @pl.loop(0, width // tile)
    def _(i):
        c = cols(i, tile)
        gz[0:length, c] = -dot(goal[...], weight[c, :], ((1,), (1,)))

    gather.round(5)
    relay(4)
    for p in range(heads // 2):
        add(p, z)
    relay(5)
    add(0, up, down)
    add(1, up, down)
    for h in range(4):
        distant(h)
    relay(6)
    add(0, far)
    add(1, far)
    add(2, up, down)
    relay(7)
    distant(4)
    distant(5)
    add(2, far)
    add(3, up, down)
    distant(6)
    distant(7)
    add(3, far)

    @pl.loop(0, heads)
    def _(h):
        c = cols(h, d)
        dq = jnp.exp((pos[...] + 1.0) * lg[h, :, 0:d] + cum[...])
        o, ot = o_buf[:, c], ot_buf[:, c]
        gzh, gzt = gz[0:length, c], gz[length:, c]
        r = lax.rsqrt(jnp.mean(o * o, axis=1, keepdims=True) + EPS)
        m = jnp.mean(o * ot, axis=1, keepdims=True)
        m1 = jnp.mean(o * gzh, axis=1, keepdims=True)
        m1t = jnp.mean(ot * gzh + o * gzt, axis=1, keepdims=True)
        r3 = r * r * r
        g = r * gzh - (r3 * m1) * o
        gt = r * gzt - (r3 * m) * gzh - (r3 * m1) * ot + (3.0 * r3 * r * r * m * m1 - r3 * m1t) * o
        g_buf[:, c] = g.astype(BF16)
        gt_buf[:, c] = gt.astype(BF16)
        gd = (dq * g).astype(BF16)
        gtd = (dq * gt).astype(BF16)
        both = dot(q[:, c], jnp.concatenate([gd, gtd], axis=1), ((0,), (0,)))
        put_state(own_b, h, per, 0, both[:, :d])
        put_state(own_b, h, per, 1, both[:, d:] + dot(qt[:, c], gd, ((0,), (0,))))

    exchange_start(n, me, own_b, recv_b, s4, r4)

    def inner_back(h):
        c = cols(h, d)
        w = weights_of(h, d, lg, dist, fall)
        dq = jnp.exp((pos[...] + 1.0) * lg[h, :, 0:d] + cum[...])
        qh, kh, vh, qth, kth, vth, g, gt = (x[:, c] for x in (q, k, v, qt, kt, vt, g_buf, gt_buf))
        a = dot(qh, kh, ((1,), (1,)))
        at = dot(jnp.concatenate([qth, qh], axis=1), jnp.concatenate([kh, kth], axis=1), ((1,), (1,)))
        p = (a * w).astype(BF16)
        pt = (at * w).astype(BF16)
        b = (dot(g, vh, ((1,), (1,))) * w).astype(BF16)
        bt = dot(jnp.concatenate([gt, g], axis=1), jnp.concatenate([vh, vth], axis=1), ((1,), (1,)))
        bt = (bt * w).astype(BF16)
        s = state_of(state, h, per, 0)
        st = state_of(state, h, per, 1)
        outer = dot(jnp.concatenate([gt, g], axis=1), jnp.concatenate([s, st], axis=1), ((1,), (1,)))
        hq[:, c] = (
            dot(jnp.concatenate([bt, b], axis=1), jnp.concatenate([kh, kth], axis=0)) + dq * outer
        ).astype(BF16)
        hk_buf[:, c] = dot(jnp.concatenate([bt, b], axis=0), jnp.concatenate([qh, qth], axis=0), ((0,), (0,)))
        hv_buf[:, c] = dot(jnp.concatenate([pt, p], axis=0), jnp.concatenate([g, gt], axis=0), ((0,), (0,)))

    pl.loop(0, heads // 2)(inner_back)
    exchange_end(n, me, own_b, recv_b, s4, r4)
    scan_slots(n, me, length, heads, lg, count, own_b, recv_b, back_b, state_b, True)
    exchange_start(n, me, back_b, state_b, s5, r5)
    pl.loop(heads // 2, heads)(inner_back)
    exchange_end(n, me, back_b, state_b, s5, r5)

    @pl.loop(0, heads)
    def _(h):
        c = cols(h, d)
        w = scale * jnp.exp((length - 1.0 - pos[...]) * lg[h, :, 0:d] + (KEPT_LOG * total - cum[...]))
        s = state_of(state_b, h, per, 0)
        st = state_of(state_b, h, per, 1)
        ks = dot(jnp.concatenate([v[:, c], vt[:, c]], axis=1), jnp.concatenate([st, s], axis=1), ((1,), (1,)))
        vs = dot(jnp.concatenate([k[:, c], kt[:, c]], axis=1), jnp.concatenate([st, s], axis=0))
        hk[:, c] = (hk_buf[:, c] + w * ks).astype(BF16)
        hv[:, c] = (hv_buf[:, c] + w * vs).astype(BF16)

    for copy in w_copies:
        copy.wait_send()
    gather.finish()

    @pl.loop(0, heads)
    def _(h):
        c = cols(h, d)
        whole, top = zall.at[z, :, c], zall.at[z, 0:length, c]
        for i, piece in enumerate((whole, whole, top, top)):
            remote(piece, piece, zs.at[h, i], zr.at[h, i], head=up).wait_send()


def on_device(n, groups, probe, source, content, probe_t, source_t, content_t, table, flags, weight, goal):
    length, width = probe.shape
    heads = table.shape[0]
    d = width // heads
    fraction = table.astype(F32) / (LEVELS - 1)
    rates = jnp.exp(math.log(1.0 / 32.0) + fraction * math.log(16.0 / (length * n)))
    lg = jnp.broadcast_to(jnp.log1p(-rates)[:, None, None], (heads, 1, length))
    flags = flags.reshape(1, length)
    vmem = pl.BlockSpec(memory_space=pltpu.VMEM)
    hbm = pl.BlockSpec(memory_space=pl.ANY)
    slots = pltpu.VMEM((n, 2 * heads * d // n, d), BF16)
    narrow, wide = pltpu.VMEM((length, width), BF16), pltpu.VMEM((length, width), F32)
    rows = width // n
    dma = pltpu.SemaphoreType.DMA
    out = jax.ShapeDtypeStruct((length, width), BF16)
    return pl.pallas_call(
        functools.partial(kernel, n, heads, groups),
        out_shape=(out, out, out),
        in_specs=[hbm] * 6 + [vmem] * 2 + [hbm] * 2,
        out_specs=[vmem] * 3,
        scratch_shapes=[
            *[narrow] * 6, pltpu.VMEM(weight.shape, BF16), pltpu.VMEM(goal.shape, BF16),
            pltpu.VMEM((length, length), F32), pltpu.VMEM((length, length), F32),
            pltpu.VMEM((length, d), F32), pltpu.VMEM((length, d), F32),
            pltpu.VMEM((1, 1, 128), F32), pltpu.VMEM((n, 1, 128), F32),
            *[slots] * 8,
            pltpu.VMEM((groups, rows, weight.shape[1]), BF16),
            pltpu.VMEM((groups, width, width), BF16),
            pltpu.VMEM((groups, 2 * length, width), BF16),
            pltpu.VMEM((2 * length, width), F32),
            wide, wide, narrow, narrow, wide, wide,
            dma((8,)), *[dma((n,))] * 10, dma((4,)), dma((4,)), dma((36,)), dma((n, 2)), dma((heads, 4)), dma((heads, 4)),
        ],
        compiler_params=pltpu.CompilerParams(collective_id=0, has_side_effects=True, vmem_limit_bytes=62 << 20),
        name="retention_hvp",
    )(probe, source, content, probe_t, source_t, content_t, lg, flags, weight, goal)


def solution(mesh):
    n, groups = mesh.shape["seq"], mesh.shape["head"]
    both = P("seq", "head")
    return jax.shard_map(
        functools.partial(on_device, n, groups),
        mesh=mesh,
        in_specs=(both,) * 6 + (P("head"), P("seq"), P("head", None), P("seq", None)),
        out_specs=(both,) * 3,
        check_vma=False,
    )
```

time: 405 us -> 104 us (0.26); the launches traced: 397 us -> 104 us
  waiting for transfers between devices: 216 us -> 0 us
  Pallas kernels: 0 us -> 96.3 us
  matrix products: 81.9 us -> 0 us
  blocking collectives: 40.9 us -> 0 us
  other arithmetic: 24.7 us -> 0.67 us
  between operations: 14.8 us -> 0.64 us
  local copies, waits for them, and re-layouts: 18.5 us -> 6.29 us
    all_gather x8 -> x0, waiting for transfers between devices: 120 us -> none  [the longest x4 71 us: carried_in(): lax.all_gather(part.astype(kind), axis)]
    pallas_call x0 -> x1, Pallas kernels: none -> 96.3 us  [on_device(): pl.pallas_call(functools.partial(kernel, n, heads, groups), out_shape=(ou...]
    psum x1 -> x0, waiting for transfers between devices: 95.4 us -> none  [on_device(): lax.psum(part_sum.astype(jnp.bfloat16), 'head').astype(jnp.float32)]
    dot_general x37 -> x0, matrix products: 81.9 us -> none  [the longest x10 20.7 us: block_out(): scores = jnp.einsum('thd,shd->hts', q, k, precision=score_prec) * scale]
    all_gather x8 -> x0, blocking collectives: 40.9 us -> none  [the longest x5 25 us: carried_in(): lax.all_gather(part.astype(kind), axis)]
    add x6 -> x0, other arithmetic: 11.1 us -> none  [the longest x1 2.89 us: reverse_combine(): later[2] + factor * earlier[2]]
    convert_element_type x12 -> x0, other arithmetic: 9.38 us -> none  [the longest x2 4.97 us: entering(): part.astype(kind)]
    unnamed x102 -> x3, local copies, waits for them, and re-layouts: 14.1 us -> 5.6 us
  transfers between devices with their start and end apart: 9 -> 0, of which waited for: 9 -> 0; matrix products, arithmetic and copies ran while one was open for 14% -> 0% of each run, Pallas kernels for 0% -> 0%
where the time goes in v1:
time: 104 us
  Pallas kernels  96.3 us (93%)
  local copies, waits for them, and re-layouts  6.29 us (6%)
    pallas_call x1, Pallas kernels, on_device(): pl.pallas_call(functools.partial(kernel, n, heads, groups), out_shape=(ou...  96.3 us
    unnamed x3, local copies, waits for them, and re-layouts  5.6 us

profile of v1, /device:TPU:1, one launch (start us, length us, event | category | flops | bytes accessed | tf_op | source)
XLA Modules:
  0.0 103.9 jit_solution(11521341344299173353)
XLA Ops:
  0.6 0.7 negate_log-plus-one_fusion
  1.3 0.7 broadcast_in_dim.2.refs_6_
  2.0 96.3 %retention_hvp.1 = (bf16[256,1024]{1,0:T(8,128)(2,1)}, bf16[256,1024]{1,0:T(8,128)(2,1)}, bf16[256,1024]{1,0:T(8,128)(2,1)}) custom-call(bf16[256,1024]{1,0:T(8,128)(2,1)} %refs_0_.1, bf16[256,1024]{1,0:T(8,128)(2,1)} %refs_1_.1, bf16[256,1024]{1,0:T(8,128)(2,1)} %refs_2_.1, bf16[256,1024]{1,0:T(8,128)(2,1)} %refs_3_.1, bf16[256,1024]{1,0:T(8,128)(2,1)} %refs_4_.1, ...), custom_call_target="tpu_custom_call" | custom-call | tf_op jit(solution)/shard_map/retention_hvp/pallas_call | solution.py:475
  98.3 1.9 %copy.16 = bf16[256,1024]{1,0:T(8,128)(2,1)} copy(bf16[256,1024]{1,0:T(8,128)(2,1)} %get-tuple-element.6) | data formatting | bytes 1048576
  100.2 1.9 %copy.17 = bf16[256,1024]{1,0:T(8,128)(2,1)} copy(bf16[256,1024]{1,0:T(8,128)(2,1)} %get-tuple-element.7) | data formatting | bytes 1048576
  102.1 1.9 %copy.18 = bf16[256,1024]{1,0:T(8,128)(2,1)} copy(bf16[256,1024]{1,0:T(8,128)(2,1)} %get-tuple-element.8) | data formatting | bytes 1048576

commit v2 on v1

v2 whole, which is shorter than its diff:
```python
import functools
import math

import jax
import jax.numpy as jnp
from jax import lax
from jax.experimental import pallas as pl
from jax.experimental.pallas import tpu as pltpu
from jax.sharding import PartitionSpec as P

LEVELS = 8
KEPT_LOG = math.log(0.7)
EPS = 1e-06
F32 = jnp.float32
BF16 = jnp.bfloat16
MESH = pl.DeviceIdType.MESH
FAR = 1e9


def dot(a, b, dims=((1,), (0,))):
    return lax.dot_general(a, b, (dims, ((), ())), preferred_element_type=F32)


def cols(h, d):
    return pl.ds(pl.multiple_of(h * d, d), d)


def decay_tables(flags_ref, dist, fall, pos, cum):
    t = dist.shape[0]
    row = lax.broadcasted_iota(jnp.int32, (t, t), 0)
    col = lax.broadcasted_iota(jnp.int32, (t, t), 1)
    flags = jnp.broadcast_to(flags_ref[...].astype(F32), (t, t))
    cum_col = jnp.sum(jnp.where(col <= row, flags, 0.0), axis=1, keepdims=True)
    flag_col = jnp.sum(jnp.where(col == row, flags, 0.0), axis=1, keepdims=True)
    cum_row = jnp.sum(jnp.where(row <= col, flag_col, 0.0), axis=0, keepdims=True)
    dist[...] = jnp.where(row >= col, (row - col).astype(F32), FAR)
    fall[...] = KEPT_LOG * (cum_col - cum_row)
    pos[...] = lax.broadcasted_iota(jnp.int32, pos.shape, 0).astype(F32)
    cum[...] = KEPT_LOG * jnp.broadcast_to(cum_col, cum.shape)


def barrier_start(n, me, up, down):
    barrier = pltpu.get_barrier_semaphore()
    for z in (up, down):
        pl.semaphore_signal(barrier, inc=1, device_id={"head": z}, device_id_type=MESH)

    @pl.loop(1, n)
    def _(step):
        pl.semaphore_signal(barrier, inc=1, device_id={"seq": lax.rem(me + step, n)}, device_id_type=MESH)


def barrier_end(n):
    pl.semaphore_wait(pltpu.get_barrier_semaphore(), n + 1)


def weights_of(h, d, lg_ref, dist, fall):
    return jnp.exp(dist[...] * lg_ref[h] + fall[...]) * (d ** -0.5)


def remote(src, dst, send_sem, recv_sem, **where):
    return pltpu.make_async_remote_copy(
        src_ref=src, dst_ref=dst, send_sem=send_sem, recv_sem=recv_sem, device_id=where, device_id_type=MESH
    )


def arrival(dst, recv_sem):
    pltpu.make_async_copy(dst, dst, recv_sem).wait()


class GramGather:
    def __init__(self, me, full, send_sem, recv_sem):
        c = lax.rem(me, 2)
        x, y = lax.rem(me // 2, 4), me // 8
        self.me, self.c, self.f, self.s = me, c, x + c * (y - x), y + c * (x - y)
        self.full, self.send_sem, self.recv_sem = full, send_sem, recv_sem
        self.rows = full.shape[1] // 32
        self.started = []

    def at(self, df, s_off, absolute=False):
        f = df if absolute else lax.rem(self.f + df + 4, 4)
        s = lax.rem(self.s + s_off + 4, 4)
        return (f * (1 + 3 * self.c) + s * (4 - 3 * self.c)) * 2 + self.c

    def view(self, piece, half=None):
        rows = pl.ds(pl.multiple_of(piece * self.rows, self.rows), self.rows)
        if half is None:
            return self.full.at[:, rows, :]
        return self.full.at[2 * half:2 * half + 2, rows, :]

    def send(self, piece, to, half=None):
        copy = remote(
            self.view(piece, half), self.view(piece, half),
            self.send_sem.at[len(self.started)], self.recv_sem.at[piece, half or 0], seq=to,
        )
        copy.start()
        self.started.append(copy)

    def wait(self, piece, half=None):
        arrival(self.view(piece, half), self.recv_sem.at[piece, half or 0])

    def spread(self, piece):
        self.send(piece, self.at(0, 1))
        self.send(piece, self.at(0, -1))
        self.send(piece, self.me + 1 - 2 * self.c)

    def round(self, k):
        if k == 0:
            self.send(self.me, self.at(1, 0))
            self.send(self.me, self.at(-1, 0))
            self.spread(self.me)
        elif k == 1:
            for step, half in ((-1, 0), (1, 1)):
                piece = self.at(step, 0)
                self.wait(piece)
                self.send(piece, self.at(-step, 0), half)
                self.spread(piece)
        elif k == 2:
            piece = self.at(2, 0)
            self.wait(piece, 0)
            self.wait(piece, 1)
            self.spread(piece)
        elif k == 3:
            for df in (0, -1, 1, 2):
                for step, half in ((-1, 0), (1, 1)):
                    piece = self.at(df, step)
                    self.wait(piece)
                    self.send(piece, self.at(0, -step), half)
                    self.send(piece, self.me + 1 - 2 * self.c)
        elif k == 4:
            for df in (0, -1, 1, 2):
                piece = self.at(df, 2)
                self.wait(piece, 0)
                self.wait(piece, 1)
                self.send(piece, self.me + 1 - 2 * self.c)
        else:

            @pl.loop(0, 16)
            def _(i):
                self.wait(2 * i + 1 - self.c)

    def finish(self):
        for copy in self.started:
            copy.wait_send()


class Scan:
    def __init__(self, me, n, heads, length, lg, count, buffers, sems, reverse):
        self.own, self.gift, self.peer, self.tot, self.recv, self.back, self.entry, self.state, self.gift2 = buffers
        self.pair_sem, self.s1, self.r1, self.s2, self.r2 = sems
        self.c, self.chip, self.chips = lax.rem(me, 2), me // 2, n // 2
        self.sibling = me + 1 - 2 * self.c
        self.half = heads // 2
        self.length, self.lg, self.count, self.reverse = length, lg, count, reverse
        self.per = self.chips // self.half
        self.rows = self.tot.shape[1] // 2
        self.d = self.tot.shape[2]

    def mine(self, i):
        return self.half * self.c + i

    def theirs(self, i):
        return self.half * (1 - self.c) + i

    def give(self):
        self.gift_copy = remote(self.gift, self.peer, self.pair_sem.at[0], self.pair_sem.at[1], seq=self.sibling)
        self.gift_copy.start()

    def decay(self, h, core):
        return jnp.exp(float(self.length) * self.lg[h, :, 0:self.d] + KEPT_LOG * self.count[2 * self.chip + core])

    def ordered(self, i, part):
        mine, peer = self.own[i, part].astype(F32), self.peer[i, part].astype(F32)
        return jnp.where(self.c == 0, mine, peer), jnp.where(self.c == 0, peer, mine)

    def combine(self):
        @pl.loop(0, self.half)
        def _(i):
            factor = self.decay(self.mine(i), 0 if self.reverse else 1)
            for part in range(2):
                first, second = self.ordered(i, part)
                total = first + factor * second if self.reverse else first * factor + second
                self.tot[pl.ds(i * self.per, self.per), part * self.rows:(part + 1) * self.rows, :] = (
                    total.astype(BF16).reshape(self.per, self.rows, self.d)
                )

    def spread(self, src, dst, send_sem, recv_sem):
        @pl.loop(1, self.chips)
        def _(step):
            p = lax.rem(self.chip + step, self.chips)
            remote(src.at[p], dst.at[self.chip], send_sem.at[p], recv_sem.at[self.chip], seq=2 * p + self.c).start()

    def collect(self, src, dst, send_sem, recv_sem):
        @pl.loop(1, self.chips)
        def _(step):
            p = lax.rem(self.chip + step, self.chips)
            remote(src.at[p], dst.at[p], send_sem.at[p], recv_sem.at[p], seq=2 * p + self.c).wait()

    def out(self):
        self.spread(self.tot, self.recv, self.s1, self.r1)

    def out_wait(self):
        self.collect(self.tot, self.recv, self.s1, self.r1)

    def scan(self):
        self.recv[self.chip] = self.tot[self.chip]
        lg = self.lg[self.mine(self.chip // self.per), :, 0:self.d]

        def step(i, run):
            p = self.chips - 1 - i if self.reverse else i
            self.back[p] = run.astype(BF16)
            factor = jnp.exp(2.0 * self.length * lg + KEPT_LOG * (self.count[2 * p] + self.count[2 * p + 1]))
            return run * factor + self.recv[p].astype(F32)

        lax.fori_loop(0, self.chips, step, jnp.zeros(self.recv.shape[1:], F32))
        self.entry[self.chip] = self.back[self.chip]

    def home(self):
        self.spread(self.back, self.entry, self.s2, self.r2)

    def home_wait(self):
        self.collect(self.back, self.entry, self.s2, self.r2)

    def settle(self):
        @pl.loop(0, self.half)
        def _(i):
            factor = self.decay(self.mine(i), 1 if self.reverse else 0)
            for part in range(2):
                first, second = self.ordered(i, part)
                edge = self.entry[pl.ds(i * self.per, self.per), part * self.rows:(part + 1) * self.rows, :]
                edge = edge.reshape(self.d, self.d).astype(F32)
                inside = factor * edge + (second if self.reverse else first)
                keep = (self.c == 1) if self.reverse else (self.c == 0)
                self.gift2[i, part] = jnp.where(keep, inside, edge).astype(BF16)
                self.state[self.mine(i), part] = jnp.where(keep, edge, inside).astype(BF16)

        spot = self.state.at[pl.ds(self.mine(0), self.half)]
        self.gift2_copy = remote(self.gift2, spot, self.pair_sem.at[2], self.pair_sem.at[3], seq=self.sibling)
        self.gift2_copy.start()

    def settle_wait(self):
        arrival(self.state.at[pl.ds(self.theirs(0), self.half)], self.pair_sem.at[3])

    def finish(self):
        self.gift_copy.wait_send()
        self.gift2_copy.wait_send()


def kernel(n, heads, groups, *refs):
    inputs, (table, flags, w_hbm, goal_hbm), (hq, hk, hv) = refs[:6], refs[6:10], refs[10:13]
    (q, k, v, qt, kt, vt, weight, goal, dist, fall, pos, cum, lg, mine, count) = refs[13:28]
    ahead, behind = refs[28:37], refs[37:46]
    (picked, gram, zall, gz, o_buf, ot_buf, g_buf, gt_buf, hk_buf, hv_buf) = refs[46:56]
    ahead_sems, behind_sems = refs[56:61], refs[61:66]
    (load_sem, cs, cr, ws, wr, gs, gr, zs, zr) = refs[66:]
    me, z = lax.axis_index("seq"), lax.axis_index("head")
    up, down = lax.rem(z + 1, groups), lax.rem(z + groups - 1, groups)
    far = lax.rem(z + 2, groups)
    length, width = q.shape
    d = width // heads
    scale = d ** -0.5
    rows = width // n
    mine_rows = pl.ds(pl.multiple_of(me * rows, rows), rows)
    sources = (*inputs, w_hbm.at[mine_rows], w_hbm, goal_hbm)
    loads = [
        pltpu.make_async_copy(src, dst, load_sem.at[i])
        for i, (src, dst) in enumerate(zip(sources, (q, k, v, qt, kt, vt, picked.at[z], weight, goal)))
    ]
    for i in (6, 1, 2, 4, 5, 0, 3, 7, 8):
        loads[i].start()
    barrier_start(n, me, up, down)

    @pl.loop(0, heads)
    def _(h):
        fraction = jnp.full((1, length), table[h], jnp.int32).astype(F32) / (LEVELS - 1)
        rates = jnp.exp(math.log(1.0 / 32.0) + fraction * math.log(16.0 / (length * n)))
        lg[h] = jnp.log1p(-rates)

    decay_tables(flags, dist, fall, pos, cum)
    total = jnp.broadcast_to(jnp.sum(flags[...].astype(F32), axis=1, keepdims=True), (1, 128))
    mine[0] = total
    count[me] = total
    forward = Scan(me, n, heads, length, lg, count, ahead, ahead_sems, False)
    backward = Scan(me, n, heads, length, lg, count, behind, behind_sems, True)
    for i in (1, 2, 4, 5):
        loads[i].wait()

    def own_state(h, target, i):
        c = cols(h, d)
        w = scale * jnp.exp((length - 1.0 - pos[...]) * lg[h, :, 0:d] + (KEPT_LOG * total - cum[...]))
        kw = (k[:, c].astype(F32) * w).astype(BF16)
        ktw = (kt[:, c].astype(F32) * w).astype(BF16)
        both = dot(kw, jnp.concatenate([v[:, c], vt[:, c]], axis=1), ((0,), (0,)))
        target[i, 0] = both[:, :d].astype(BF16)
        target[i, 1] = (both[:, d:] + dot(ktw, v[:, c], ((0,), (0,)))).astype(BF16)

    pl.loop(0, heads // 2)(lambda i: own_state(forward.theirs(i), forward.gift, i))
    loads[6].wait()
    barrier_end(n)
    half = rows // 2
    w_copies = [
        remote(picked.at[z], picked.at[z], ws.at[0], wr.at[0], head=up),
        remote(picked.at[z], picked.at[z], ws.at[1], wr.at[1], head=down),
    ]
    for copy in w_copies:
        copy.start()
    remote(mine.at[0], count.at[me], cs.at[forward.sibling], cr.at[me], seq=forward.sibling).start()
    forward.give()

    @pl.loop(1, n)
    def _(step):
        j = lax.rem(me + step, n)

        @pl.when(j != forward.sibling)
        def _():
            remote(mine.at[0], count.at[me], cs.at[j], cr.at[me], seq=j).start()

    pl.loop(0, heads // 2)(lambda i: own_state(forward.mine(i), forward.own, i))
    arrival(count.at[forward.sibling], cr.at[forward.sibling])
    arrival(forward.peer, forward.pair_sem.at[1])
    forward.combine()
    forward.out()
    loads[0].wait()
    loads[3].wait()

    def inner(h):
        c = cols(h, d)
        w = weights_of(h, d, lg, dist, fall)
        a = dot(q[:, c], k[:, c], ((1,), (1,)))
        at = dot(
            jnp.concatenate([qt[:, c], q[:, c]], axis=1), jnp.concatenate([k[:, c], kt[:, c]], axis=1), ((1,), (1,))
        )
        p = (a * w).astype(BF16)
        pt = (at * w).astype(BF16)
        both = dot(p, jnp.concatenate([v[:, c], vt[:, c]], axis=1))
        o_buf[:, c] = both[:, :d]
        ot_buf[:, c] = both[:, d:] + dot(pt, v[:, c])

    pl.loop(0, heads // 2)(inner)
    @pl.loop(1, n)
    def _(step):
        j = lax.rem(me + step, n)

        @pl.when(j != forward.sibling)
        def _():
            arrival(count.at[j], cr.at[j])

    forward.out_wait()
    forward.scan()
    forward.home()
    arrival(picked.at[down], wr.at[0])
    w_copies.append(remote(picked.at[down, 0:half], picked.at[down, 0:half], ws.at[2], wr.at[2], head=up))
    w_copies[2].start()
    arrival(picked.at[up], wr.at[1])
    w_copies.append(remote(picked.at[up, half:rows], picked.at[up, half:rows], ws.at[3], wr.at[3], head=down))
    w_copies[3].start()
    pl.loop(heads // 2, heads)(inner)
    forward.home_wait()
    forward.settle()

    def z_send(i):
        c = cols(lax.rem(forward.mine(i), heads), d)
        remote(zall.at[z, :, c], zall.at[z, :, c], zs.at[i, 0], zr.at[i, 0], head=up).start()
        remote(zall.at[z, :, c], zall.at[z, :, c], zs.at[i, 1], zr.at[i, 1], head=down).start()

    def output(i):
        h = lax.rem(forward.mine(i), heads)
        c = cols(h, d)
        dq = jnp.exp((pos[...] + 1.0) * lg[h, :, 0:d] + cum[...])
        s, st = forward.state[h, 0], forward.state[h, 1]
        both = dot(q[:, c], jnp.concatenate([s, st], axis=1))
        o = o_buf[:, c] + dq * both[:, :d]
        ot = ot_buf[:, c] + dq * (both[:, d:] + dot(qt[:, c], s))
        o_buf[:, c] = o
        ot_buf[:, c] = ot
        r = lax.rsqrt(jnp.mean(o * o, axis=1, keepdims=True) + EPS)
        m = jnp.mean(o * ot, axis=1, keepdims=True)
        zall[z, 0:length, c] = (o * r).astype(BF16)
        zall[z, length:, c] = (r * ot - o * (r * r * r * m)).astype(BF16)

        @pl.when(i > 0)
        def _():
            z_send(i - 1)

    pl.loop(0, heads // 2)(output)
    forward.settle_wait()
    pl.loop(heads // 2, heads)(output)
    z_send(heads - 1)
    arrival(picked.at[far, 0:half], wr.at[2])
    arrival(picked.at[far, half:rows], wr.at[3])
    loads[7].wait()
    tile = 256

    @pl.loop(0, width // tile)
    def _(i):
        c = cols(i, tile)
        part = dot(picked[...].reshape(groups * rows, weight.shape[1]), weight[c, :], ((1,), (1,)))
        gram[:, mine_rows, c] = part.astype(BF16).reshape(groups, rows, tile)

    loads[8].wait()

    def goal_tile(i):
        c = slice(i * tile, (i + 1) * tile)
        gz[0:length, c] = -dot(goal[...], weight[c, :], ((1,), (1,)))

    def chunk(i):
        return cols(lax.rem(forward.mine(i), heads), d)

    def relay(i):
        c = chunk(i)
        arrival(zall.at[down, :, c], zr.at[i, 0])
        remote(zall.at[down, 0:length, c], zall.at[down, 0:length, c], zs.at[i, 2], zr.at[i, 2], head=up).start()
        arrival(zall.at[up, :, c], zr.at[i, 1])
        remote(zall.at[up, length:, c], zall.at[up, length:, c], zs.at[i, 3], zr.at[i, 3], head=down).start()

    def distant(i):
        c = chunk(i)
        arrival(zall.at[far, 0:length, c], zr.at[i, 2])
        arrival(zall.at[far, length:, c], zr.at[i, 3])

    def add(first, number, *sources):
        part = pl.ds(pl.multiple_of(lax.rem(forward.mine(first), heads) * d, 2 * d), number * d)

        @pl.loop(0, width // tile)
        def _(i):
            c = cols(i, tile)
            value = gz[:, c]
            for g in sources:
                value = value + dot(zall[g, :, part], gram[g, part, c])
            gz[:, c] = value

    gather = GramGather(me, gram, gs, gr)
    gather.round(0)
    goal_tile(0)
    goal_tile(1)
    gather.round(1)
    relay(0)
    goal_tile(2)
    gather.round(2)
    relay(1)
    goal_tile(3)
    gather.round(3)
    relay(2)
    gather.round(4)
    relay(3)
    gather.round(5)
    relay(4)

    @pl.loop(0, width // tile)
    def _(i):
        c = cols(i, tile)
        gz[0:length, c] = gz[0:length, c] + dot(zall[z, 0:length, :], gram[z, :, c])
        gz[length:, c] = dot(zall[z, length:, :], gram[z, :, c])

    relay(5)
    add(0, 4, up, down)
    relay(6)
    for i in range(4):
        distant(i)
    add(0, 4, far)
    add(4, 2, up, down)
    relay(7)
    distant(4)
    distant(5)
    add(4, 2, far)
    add(6, 2, up, down)
    distant(6)
    distant(7)
    add(6, 2, far)

    def norm_back(h, target, i):
        c = cols(h, d)
        dq = jnp.exp((pos[...] + 1.0) * lg[h, :, 0:d] + cum[...])
        o, ot = o_buf[:, c], ot_buf[:, c]
        gzh, gzt = gz[0:length, c], gz[length:, c]
        r = lax.rsqrt(jnp.mean(o * o, axis=1, keepdims=True) + EPS)
        m = jnp.mean(o * ot, axis=1, keepdims=True)
        m1 = jnp.mean(o * gzh, axis=1, keepdims=True)
        m1t = jnp.mean(ot * gzh + o * gzt, axis=1, keepdims=True)
        r3 = r * r * r
        g = r * gzh - (r3 * m1) * o
        gt = r * gzt - (r3 * m) * gzh - (r3 * m1) * ot + (3.0 * r3 * r * r * m * m1 - r3 * m1t) * o
        g_buf[:, c] = g.astype(BF16)
        gt_buf[:, c] = gt.astype(BF16)
        gd = (dq * g).astype(BF16)
        gtd = (dq * gt).astype(BF16)
        both = dot(q[:, c], jnp.concatenate([gd, gtd], axis=1), ((0,), (0,)))
        target[i, 0] = both[:, :d].astype(BF16)
        target[i, 1] = (both[:, d:] + dot(qt[:, c], gd, ((0,), (0,)))).astype(BF16)

    pl.loop(0, heads // 2)(lambda i: norm_back(backward.theirs(i), backward.gift, i))
    backward.give()
    pl.loop(0, heads // 2)(lambda i: norm_back(backward.mine(i), backward.own, i))
    arrival(backward.peer, backward.pair_sem.at[1])
    backward.combine()
    backward.out()

    def inner_back(h):
        c = cols(h, d)
        w = weights_of(h, d, lg, dist, fall)
        dq = jnp.exp((pos[...] + 1.0) * lg[h, :, 0:d] + cum[...])
        qh, kh, vh, qth, kth, vth, g, gt = (x[:, c] for x in (q, k, v, qt, kt, vt, g_buf, gt_buf))
        a = dot(qh, kh, ((1,), (1,)))
        at = dot(jnp.concatenate([qth, qh], axis=1), jnp.concatenate([kh, kth], axis=1), ((1,), (1,)))
        p = (a * w).astype(BF16)
        pt = (at * w).astype(BF16)
        b = (dot(g, vh, ((1,), (1,))) * w).astype(BF16)
        bt = dot(jnp.concatenate([gt, g], axis=1), jnp.concatenate([vh, vth], axis=1), ((1,), (1,)))
        bt = (bt * w).astype(BF16)
        s, st = forward.state[h, 0], forward.state[h, 1]
        outer = dot(jnp.concatenate([gt, g], axis=1), jnp.concatenate([s, st], axis=1), ((1,), (1,)))
        hq[:, c] = (
            dot(jnp.concatenate([bt, b], axis=1), jnp.concatenate([kh, kth], axis=0)) + dq * outer
        ).astype(BF16)
        hk_buf[:, c] = dot(jnp.concatenate([bt, b], axis=0), jnp.concatenate([qh, qth], axis=0), ((0,), (0,)))
        hv_buf[:, c] = dot(jnp.concatenate([pt, p], axis=0), jnp.concatenate([g, gt], axis=0), ((0,), (0,)))

    pl.loop(0, heads // 2)(inner_back)
    backward.out_wait()
    backward.scan()
    backward.home()
    pl.loop(heads // 2, heads)(inner_back)
    backward.home_wait()
    backward.settle()

    def last(i):
        h = lax.rem(backward.mine(i), heads)
        c = cols(h, d)
        w = scale * jnp.exp((length - 1.0 - pos[...]) * lg[h, :, 0:d] + (KEPT_LOG * total - cum[...]))
        s, st = backward.state[h, 0], backward.state[h, 1]
        ks = dot(jnp.concatenate([v[:, c], vt[:, c]], axis=1), jnp.concatenate([st, s], axis=1), ((1,), (1,)))
        vs = dot(jnp.concatenate([k[:, c], kt[:, c]], axis=1), jnp.concatenate([st, s], axis=0))
        hk[:, c] = (hk_buf[:, c] + w * ks).astype(BF16)
        hv[:, c] = (hv_buf[:, c] + w * vs).astype(BF16)

    pl.loop(0, heads // 2)(last)
    backward.settle_wait()
    pl.loop(heads // 2, heads)(last)
    forward.finish()
    backward.finish()
    for copy in w_copies:
        copy.wait_send()
    gather.finish()

    @pl.loop(1, n)
    def _(step):
        j = lax.rem(me + step, n)
        remote(mine.at[0], count.at[me], cs.at[j], cr.at[me], seq=j).wait_send()

    @pl.loop(0, heads)
    def _(i):
        c = cols(i, d)
        whole, top = zall.at[z, :, c], zall.at[z, 0:length, c]
        for kind, piece in enumerate((whole, whole, top, top)):
            remote(piece, piece, zs.at[i, kind], zr.at[i, kind], head=up).wait_send()


def store_kernel(*refs):
    copies = [pltpu.make_async_copy(refs[i], refs[3 + i], refs[6].at[i]) for i in range(3)]
    for copy in copies:
        copy.start()
    for copy in copies:
        copy.wait()


def on_device(n, groups, probe, source, content, probe_t, source_t, content_t, table, flags, weight, goal):
    length, width = probe.shape
    heads = table.shape[0]
    d = width // heads
    flags = flags.reshape(1, length)
    vmem, smem, hbm = (pl.BlockSpec(memory_space=m) for m in (pltpu.VMEM, pltpu.SMEM, pltpu.HBM))
    pair = pltpu.VMEM((heads // 2, 2, d, d), BF16)
    slots = pltpu.VMEM((n // 2, 2 * heads * d // n, d), BF16)
    scan = [pair, pair, pair, slots, slots, slots, slots, pltpu.VMEM((heads, 2, d, d), BF16), pair]
    narrow, wide = pltpu.VMEM((length, width), BF16), pltpu.VMEM((length, width), F32)
    rows = width // n
    dma = pltpu.SemaphoreType.DMA
    out = jax.ShapeDtypeStruct((length, width), BF16)
    results = pl.pallas_call(
        functools.partial(kernel, n, heads, groups),
        out_shape=(out, out, out),
        in_specs=[hbm] * 6 + [smem, vmem] + [hbm] * 2,
        out_specs=[vmem] * 3,
        scratch_shapes=[
            *[narrow] * 6, pltpu.VMEM(weight.shape, BF16), pltpu.VMEM(goal.shape, BF16),
            pltpu.VMEM((length, length), F32), pltpu.VMEM((length, length), F32),
            pltpu.VMEM((length, d), F32), pltpu.VMEM((length, d), F32),
            pltpu.VMEM((heads, 1, length), F32), pltpu.VMEM((1, 1, d), F32), pltpu.VMEM((n, 1, d), F32),
            *scan, *scan,
            pltpu.VMEM((groups, rows, weight.shape[1]), BF16),
            pltpu.VMEM((groups, width, width), BF16),
            pltpu.VMEM((groups, 2 * length, width), BF16),
            pltpu.VMEM((2 * length, width), F32),
            wide, wide, narrow, narrow, wide, wide,
            *([dma((4,))] + [dma((n // 2,))] * 4) * 2,
            dma((9,)), dma((n,)), dma((n,)), dma((4,)), dma((4,)), dma((36,)), dma((n, 2)), dma((heads, 4)), dma((heads, 4)),
        ],
        compiler_params=pltpu.CompilerParams(collective_id=0, has_side_effects=True, vmem_limit_bytes=52 << 20),
        name="retention_hvp",
    )(probe, source, content, probe_t, source_t, content_t, table, flags, weight, goal)
    return pl.pallas_call(
        store_kernel,
        out_shape=(out, out, out),
        in_specs=[vmem] * 3,
        out_specs=[hbm] * 3,
        scratch_shapes=[dma((3,))],
        compiler_params=pltpu.CompilerParams(vmem_limit_bytes=4 << 20),
        name="store",
    )(*results)


def solution(mesh):
    n, groups = mesh.shape["seq"], mesh.shape["head"]
    both = P("seq", "head")
    return jax.shard_map(
        functools.partial(on_device, n, groups),
        mesh=mesh,
        in_specs=(both,) * 6 + (P("head"), P("seq"), P("head", None), P("seq", None)),
        out_specs=(both,) * 3,
        check_vma=False,
    )
```

time: 104 us -> 93.1 us (0.90)
  Pallas kernels: 96.3 us -> 91 us
  local copies, waits for them, and re-layouts: 6.29 us -> 1.33 us
    pallas_call x1, Pallas kernels: 96.3 us -> 89.8 us  [on_device(): pl.pallas_call(functools.partial(kernel, n, heads, groups), out_shape=(ou...]
    unnamed x3 -> x4, local copies, waits for them, and re-layouts: 5.6 us -> 1.33 us
    pallas_call x0 -> x1, Pallas kernels: none -> 1.17 us  [on_device(): pl.pallas_call(store_kernel, out_shape=(out, out, out), in_specs=[vmem] *...]
where the time goes in v2:
time: 93.1 us; the launch traced here: 93 us
  Pallas kernels  91 us (98%)
  local copies, waits for them, and re-layouts  1.33 us (1%)
    pallas_call x1, Pallas kernels, on_device(): pl.pallas_call(functools.partial(kernel, n, heads, groups), out_shape=(ou...  89.8 us

profile of v2, /device:TPU:1, one launch (start us, length us, event | category | flops | bytes accessed | tf_op | source)
XLA Modules:
  0.0 93.0 jit_solution(13110931640918547806)
XLA Ops:
  0.6 0.0 copy-start
  0.6 0.7 copy-done
  1.3 0.0 copy-start.1
  1.3 0.7 copy-done.1
  2.0 89.8 %retention_hvp.1 = (bf16[256,1024]{1,0:T(8,128)(2,1)S(1)}, bf16[256,1024]{1,0:T(8,128)(2,1)S(1)}, bf16[256,1024]{1,0:T(8,128)(2,1)S(1)}) custom-call(bf16[256,1024]{1,0:T(8,128)(2,1)} %refs_0_.1, bf16[256,1024]{1,0:T(8,128)(2,1)} %refs_1_.1, bf16[256,1024]{1,0:T(8,128)(2,1)} %refs_2_.1, bf16[256,1024]{1,0:T(8,128)(2,1)} %refs_3_.1, ...), custom_call_target="tpu_custom_call" | custom-call | tf_op jit(solution)/shard_map/retention_hvp/pallas_call | solution.py:578
  91.8 1.2 %store.1 = (bf16[256,1024]{1,0:T(8,128)(2,1)}, bf16[256,1024]{1,0:T(8,128)(2,1)}, bf16[256,1024]{1,0:T(8,128)(2,1)}) custom-call(bf16[256,1024]{1,0:T(8,128)(2,1)S(1)} %get-tuple-element.6.refs_0_, bf16[256,1024]{1,0:T(8,128)(2,1)S(1)} %get-tuple-element.7.refs_1_, bf16[256,1024]{1,0:T(8,128)(2,1)S(1)} %get-tuple-element.8.refs_2_), custom_call_target="tpu_custom_call" | custom-call | tf_op jit(solution)/shard_map/store/pallas_call | solution.py:600
Async XLA Ops:
  0.6 0.7 copy-start
  1.3 0.7 copy-start.1

commit v3 on v2

--- a/solution.py
+++ b/solution.py
@@ -15,6 +15,7 @@
 BF16 = jnp.bfloat16
 MESH = pl.DeviceIdType.MESH
 FAR = 1e9
+UNROLL = 2
 
 
 def dot(a, b, dims=((1,), (0,))):
@@ -74,7 +75,6 @@
         self.me, self.c, self.f, self.s = me, c, x + c * (y - x), y + c * (x - y)
         self.full, self.send_sem, self.recv_sem = full, send_sem, recv_sem
         self.rows = full.shape[1] // 32
-        self.started = []
 
     def at(self, df, s_off, absolute=False):
         f = df if absolute else lax.rem(self.f + df + 4, 4)
@@ -87,66 +87,71 @@
             return self.full.at[:, rows, :]
         return self.full.at[2 * half:2 * half + 2, rows, :]
 
-    def send(self, piece, to, half=None):
-        copy = remote(
-            self.view(piece, half), self.view(piece, half),
-            self.send_sem.at[len(self.started)], self.recv_sem.at[piece, half or 0], seq=to,
-        )
-        copy.start()
-        self.started.append(copy)
-
-    def wait(self, piece, half=None):
-        arrival(self.view(piece, half), self.recv_sem.at[piece, half or 0])
-
-    def spread(self, piece):
-        self.send(piece, self.at(0, 1))
-        self.send(piece, self.at(0, -1))
-        self.send(piece, self.me + 1 - 2 * self.c)
+    def send(self, piece, to, lane, half=None):
+        view = self.view(piece, half)
+        remote(view, view, self.send_sem.at[0], self.recv_sem.at[lane], seq=to).start()
+
+    def wait(self, piece, lane):
+        arrival(self.view(piece), self.recv_sem.at[lane])
+
+    def spread(self, piece, df):
+        self.send(piece, self.at(0, 1), self.lane(-1, df))
+        self.send(piece, self.at(0, -1), self.lane(1, df))
+        self.sideways(piece)
+
+    def sideways(self, piece):
+        self.send(piece, self.me + 1 - 2 * self.c, 12)
+
+    def lane(self, step, df):
+        return 3 + (4 if step == 1 else 0) + df % 4
+
+    def pass_on(self, step, df, half):
+        piece = self.at(df, step)
+        self.wait(piece, self.lane(step, df))
+        self.send(piece, self.at(0, -step), 11, half)
+        self.sideways(piece)
 
     def round(self, k):
         if k == 0:
-            self.send(self.me, self.at(1, 0))
-            self.send(self.me, self.at(-1, 0))
-            self.spread(self.me)
+            self.send(self.me, self.at(1, 0), 0)
+            self.send(self.me, self.at(-1, 0), 1)
+            self.spread(self.me, 0)
         elif k == 1:
             for step, half in ((-1, 0), (1, 1)):
-                piece = self.at(step, 0)
-                self.wait(piece)
-                self.send(piece, self.at(-step, 0), half)
-                self.spread(piece)
+                self.wait(self.at(step, 0), half)
+                self.send(self.at(step, 0), self.at(-step, 0), 2, half)
+            for step in (-1, 1):
+                self.spread(self.at(step, 0), step)
+            for step, half in ((-1, 0), (1, 1)):
+                self.pass_on(step, 0, half)
         elif k == 2:
-            piece = self.at(2, 0)
-            self.wait(piece, 0)
-            self.wait(piece, 1)
-            self.spread(piece)
+            self.wait(self.at(2, 0), 2)
+            self.spread(self.at(2, 0), 2)
         elif k == 3:
-            for df in (0, -1, 1, 2):
+            for df in (-1, 1):
                 for step, half in ((-1, 0), (1, 1)):
-                    piece = self.at(df, step)
-                    self.wait(piece)
-                    self.send(piece, self.at(0, -step), half)
-                    self.send(piece, self.me + 1 - 2 * self.c)
+                    self.pass_on(step, df, half)
         elif k == 4:
-            for df in (0, -1, 1, 2):
-                piece = self.at(df, 2)
-                self.wait(piece, 0)
-                self.wait(piece, 1)
-                self.send(piece, self.me + 1 - 2 * self.c)
+            for step, half in ((-1, 0), (1, 1)):
+                self.pass_on(step, 2, half)
+        elif k == 5:
+            four = self.full.at[:, 0:4 * self.rows, :]
+            arrival(four, self.recv_sem.at[11])
+            for df in range(4):
+                self.sideways(self.at(df, 2))
         else:
-
-            @pl.loop(0, 16)
-            def _(i):
-                self.wait(2 * i + 1 - self.c)
+            arrival(self.full.at[:, 0:16 * self.rows, :], self.recv_sem.at[12])
 
     def finish(self):
-        for copy in self.started:
-            copy.wait_send()
+        sent = self.full.at[:, 0:31 * self.rows, :]
+        pltpu.make_async_copy(sent, sent, self.send_sem.at[0]).wait()
 
 
 class Scan:
     def __init__(self, me, n, heads, length, lg, count, buffers, sems, reverse):
         self.own, self.gift, self.peer, self.tot, self.recv, self.back, self.entry, self.state, self.gift2 = buffers
-        self.pair_sem, self.s1, self.r1, self.s2, self.r2 = sems
+        self.pair_sem, hop_sem = sems
+        self.s1, self.r1, self.s2, self.r2 = (hop_sem.at[i] for i in range(4))
         self.c, self.chip, self.chips = lax.rem(me, 2), me // 2, n // 2
         self.sibling = me + 1 - 2 * self.c
         self.half = heads // 2
@@ -187,13 +192,12 @@
         @pl.loop(1, self.chips)
         def _(step):
             p = lax.rem(self.chip + step, self.chips)
-            remote(src.at[p], dst.at[self.chip], send_sem.at[p], recv_sem.at[self.chip], seq=2 * p + self.c).start()
+            remote(src.at[p], dst.at[self.chip], send_sem, recv_sem, seq=2 * p + self.c).start()
 
     def collect(self, src, dst, send_sem, recv_sem):
-        @pl.loop(1, self.chips)
-        def _(step):
-            p = lax.rem(self.chip + step, self.chips)
-            remote(src.at[p], dst.at[p], send_sem.at[p], recv_sem.at[p], seq=2 * p + self.c).wait()
+        sent, got = src.at[0:self.chips - 1], dst.at[0:self.chips - 1]
+        pltpu.make_async_copy(sent, sent, send_sem).wait()
+        arrival(got, recv_sem)
 
     def out(self):
         self.spread(self.tot, self.recv, self.s1, self.r1)
@@ -233,25 +237,31 @@
                 self.gift2[i, part] = jnp.where(keep, inside, edge).astype(BF16)
                 self.state[self.mine(i), part] = jnp.where(keep, edge, inside).astype(BF16)
 
-        spot = self.state.at[pl.ds(self.mine(0), self.half)]
-        self.gift2_copy = remote(self.gift2, spot, self.pair_sem.at[2], self.pair_sem.at[3], seq=self.sibling)
-        self.gift2_copy.start()
-
-    def settle_wait(self):
-        arrival(self.state.at[pl.ds(self.theirs(0), self.half)], self.pair_sem.at[3])
+        self.gift2_copies = [
+            remote(
+                self.gift2.at[i], self.state.at[self.mine(i)],
+                self.pair_sem.at[2], self.pair_sem.at[3 + i], seq=self.sibling,
+            )
+            for i in range(self.half)
+        ]
+        for copy in self.gift2_copies:
+            copy.start()
+
+    def settle_wait(self, i):
+        arrival(self.state.at[self.theirs(i)], self.pair_sem.at[3 + i])
 
     def finish(self):
-        self.gift_copy.wait_send()
-        self.gift2_copy.wait_send()
+        pltpu.make_async_copy(self.gift2, self.gift2, self.pair_sem.at[2]).wait()
 
 
 def kernel(n, heads, groups, *refs):
-    inputs, (table, flags, w_hbm, goal_hbm), (hq, hk, hv) = refs[:6], refs[6:10], refs[10:13]
+    inputs, (table_hbm, flags_hbm, w_hbm, goal_hbm), results = refs[:6], refs[6:10], refs[10:13]
     (q, k, v, qt, kt, vt, weight, goal, dist, fall, pos, cum, lg, mine, count) = refs[13:28]
     ahead, behind = refs[28:37], refs[37:46]
     (picked, gram, zall, gz, o_buf, ot_buf, g_buf, gt_buf, hk_buf, hv_buf) = refs[46:56]
-    ahead_sems, behind_sems = refs[56:61], refs[61:66]
-    (load_sem, cs, cr, ws, wr, gs, gr, zs, zr) = refs[66:]
+    ahead_sems, behind_sems = refs[56:58], refs[58:60]
+    (load_sem, cs, cr, ws, wr, gs, gr, zs, zr) = refs[60:69]
+    (hq, hk, hv, g_rest, gt_rest, table, flags, out_sem) = refs[69:]
     me, z = lax.axis_index("seq"), lax.axis_index("head")
     up, down = lax.rem(z + 1, groups), lax.rem(z + groups - 1, groups)
     far = lax.rem(z + 2, groups)
@@ -260,14 +270,16 @@
     scale = d ** -0.5
     rows = width // n
     mine_rows = pl.ds(pl.multiple_of(me * rows, rows), rows)
-    sources = (*inputs, w_hbm.at[mine_rows], w_hbm, goal_hbm)
+    sources = (*inputs, w_hbm.at[mine_rows], w_hbm, goal_hbm, table_hbm, flags_hbm)
     loads = [
         pltpu.make_async_copy(src, dst, load_sem.at[i])
-        for i, (src, dst) in enumerate(zip(sources, (q, k, v, qt, kt, vt, picked.at[z], weight, goal)))
+        for i, (src, dst) in enumerate(zip(sources, (q, k, v, qt, kt, vt, picked.at[z], weight, goal, table, flags)))
     ]
-    for i in (6, 1, 2, 4, 5, 0, 3, 7, 8):
+    for i in (9, 10, 6, 1, 2, 4, 5, 0, 3, 7, 8):
         loads[i].start()
     barrier_start(n, me, up, down)
+    loads[9].wait()
+    loads[10].wait()
 
     @pl.loop(0, heads)
     def _(h):
@@ -293,29 +305,24 @@
         target[i, 0] = both[:, :d].astype(BF16)
         target[i, 1] = (both[:, d:] + dot(ktw, v[:, c], ((0,), (0,)))).astype(BF16)
 
-    pl.loop(0, heads // 2)(lambda i: own_state(forward.theirs(i), forward.gift, i))
     loads[6].wait()
     barrier_end(n)
     half = rows // 2
-    w_copies = [
-        remote(picked.at[z], picked.at[z], ws.at[0], wr.at[0], head=up),
-        remote(picked.at[z], picked.at[z], ws.at[1], wr.at[1], head=down),
-    ]
-    for copy in w_copies:
-        copy.start()
-    remote(mine.at[0], count.at[me], cs.at[forward.sibling], cr.at[me], seq=forward.sibling).start()
+    low, high = slice(0, half), slice(half, rows)
+
+    def w_send(slot, part, lane, to):
+        remote(picked.at[slot, part], picked.at[slot, part], ws.at[0], wr.at[lane], head=to).start()
+
+    w_send(z, low, 0, up)
+    w_send(z, high, 1, down)
+    w_send(z, high, 2, up)
+    w_send(z, low, 2, down)
+    pl.loop(0, heads // 2, unroll=UNROLL)(lambda i: own_state(forward.theirs(i), forward.gift, i))
+    remote(mine.at[0], count.at[me], cs.at[0], cr.at[0], seq=forward.sibling).start()
     forward.give()
 
-    @pl.loop(1, n)
-    def _(step):
-        j = lax.rem(me + step, n)
-
-        @pl.when(j != forward.sibling)
-        def _():
-            remote(mine.at[0], count.at[me], cs.at[j], cr.at[me], seq=j).start()
-
-    pl.loop(0, heads // 2)(lambda i: own_state(forward.mine(i), forward.own, i))
-    arrival(count.at[forward.sibling], cr.at[forward.sibling])
+    pl.loop(0, heads // 2, unroll=UNROLL)(lambda i: own_state(forward.mine(i), forward.own, i))
+    arrival(count.at[forward.sibling], cr.at[0])
     arrival(forward.peer, forward.pair_sem.at[1])
     forward.combine()
     forward.out()
@@ -335,32 +342,43 @@
         o_buf[:, c] = both[:, :d]
         ot_buf[:, c] = both[:, d:] + dot(pt, v[:, c])
 
-    pl.loop(0, heads // 2)(inner)
     @pl.loop(1, n)
     def _(step):
         j = lax.rem(me + step, n)
 
         @pl.when(j != forward.sibling)
         def _():
-            arrival(count.at[j], cr.at[j])
-
+            remote(mine.at[0], count.at[me], cs.at[0], cr.at[1], seq=j).start()
+
+    pl.loop(0, heads // 2)(inner)
+    arrival(picked.at[down, low], wr.at[0])
+    w_send(down, low, 2, up)
+    arrival(picked.at[up, high], wr.at[1])
+    w_send(up, high, 2, down)
+    arrival(count.at[0:n - 2], cr.at[1])
     forward.out_wait()
     forward.scan()
     forward.home()
-    arrival(picked.at[down], wr.at[0])
-    w_copies.append(remote(picked.at[down, 0:half], picked.at[down, 0:half], ws.at[2], wr.at[2], head=up))
-    w_copies[2].start()
-    arrival(picked.at[up], wr.at[1])
-    w_copies.append(remote(picked.at[up, half:rows], picked.at[up, half:rows], ws.at[3], wr.at[3], head=down))
-    w_copies[3].start()
     pl.loop(heads // 2, heads)(inner)
+    arrival(picked.at[0:2], wr.at[2])
+    loads[7].wait()
+    tile = 256
+
+    @pl.loop(0, width // tile)
+    def _(i):
+        c = cols(i, tile)
+        part = dot(picked[...].reshape(groups * rows, weight.shape[1]), weight[c, :], ((1,), (1,)))
+        gram[:, mine_rows, c] = part.astype(BF16).reshape(groups, rows, tile)
+
+    gather = GramGather(me, gram, gs, gr)
     forward.home_wait()
     forward.settle()
+    gather.round(0)
 
     def z_send(i):
         c = cols(lax.rem(forward.mine(i), heads), d)
-        remote(zall.at[z, :, c], zall.at[z, :, c], zs.at[i, 0], zr.at[i, 0], head=up).start()
-        remote(zall.at[z, :, c], zall.at[z, :, c], zs.at[i, 1], zr.at[i, 1], head=down).start()
+        remote(zall.at[z, :, c], zall.at[z, :, c], zs.at[0], zr.at[2 * i], head=up).start()
+        remote(zall.at[z, :, c], zall.at[z, :, c], zs.at[0], zr.at[2 * i + 1], head=down).start()
 
     def output(i):
         h = lax.rem(forward.mine(i), heads)
@@ -377,25 +395,16 @@
         zall[z, 0:length, c] = (o * r).astype(BF16)
         zall[z, length:, c] = (r * ot - o * (r * r * r * m)).astype(BF16)
 
-        @pl.when(i > 0)
-        def _():
+        if isinstance(i, int):
             z_send(i - 1)
+        else:
+            pl.when(i > 0)(lambda: z_send(i - 1))
 
     pl.loop(0, heads // 2)(output)
-    forward.settle_wait()
-    pl.loop(heads // 2, heads)(output)
+    for i in range(heads // 2, heads):
+        forward.settle_wait(i - heads // 2)
+        output(i)
     z_send(heads - 1)
-    arrival(picked.at[far, 0:half], wr.at[2])
-    arrival(picked.at[far, half:rows], wr.at[3])
-    loads[7].wait()
-    tile = 256
-
-    @pl.loop(0, width // tile)
-    def _(i):
-        c = cols(i, tile)
-        part = dot(picked[...].reshape(groups * rows, weight.shape[1]), weight[c, :], ((1,), (1,)))
-        gram[:, mine_rows, c] = part.astype(BF16).reshape(groups, rows, tile)
-
     loads[8].wait()
 
     def goal_tile(i):
@@ -405,66 +414,64 @@
     def chunk(i):
         return cols(lax.rem(forward.mine(i), heads), d)
 
+    groups_of = (0, 0, 0, 0, 1, 1, 2, 2)
+
     def relay(i):
         c = chunk(i)
-        arrival(zall.at[down, :, c], zr.at[i, 0])
-        remote(zall.at[down, 0:length, c], zall.at[down, 0:length, c], zs.at[i, 2], zr.at[i, 2], head=up).start()
-        arrival(zall.at[up, :, c], zr.at[i, 1])
-        remote(zall.at[up, length:, c], zall.at[up, length:, c], zs.at[i, 3], zr.at[i, 3], head=down).start()
-
-    def distant(i):
-        c = chunk(i)
-        arrival(zall.at[far, 0:length, c], zr.at[i, 2])
-        arrival(zall.at[far, length:, c], zr.at[i, 3])
+        lane = 2 * heads + groups_of[i]
+        arrival(zall.at[down, :, c], zr.at[2 * i])
+        piece = zall.at[down, 0:length, c]
+        remote(piece, piece, zs.at[0], zr.at[lane], head=up).start()
+        arrival(zall.at[up, :, c], zr.at[2 * i + 1])
+        piece = zall.at[up, length:, c]
+        remote(piece, piece, zs.at[0], zr.at[lane], head=down).start()
+
+    def span(first, number):
+        return pl.ds(pl.multiple_of(lax.rem(forward.mine(first), heads) * d, number * d), number * d)
+
+    def distant(first, number):
+        arrival(zall.at[far, :, span(first, number)], zr.at[2 * heads + groups_of[first]])
 
     def add(first, number, *sources):
-        part = pl.ds(pl.multiple_of(lax.rem(forward.mine(first), heads) * d, 2 * d), number * d)
+        part = span(first, number)
 
         @pl.loop(0, width // tile)
         def _(i):
             c = cols(i, tile)
-            value = gz[:, c]
-            for g in sources:
-                value = value + dot(zall[g, :, part], gram[g, part, c])
-            gz[:, c] = value
-
-    gather = GramGather(me, gram, gs, gr)
-    gather.round(0)
+            for r in (slice(0, length), slice(length, 2 * length)):
+                gz[r, c] = sum((dot(zall[g, r, part], gram[g, part, c]) for g in sources), gz[r, c])
+
     goal_tile(0)
     goal_tile(1)
     gather.round(1)
     relay(0)
     goal_tile(2)
+    relay(1)
     gather.round(2)
-    relay(1)
     goal_tile(3)
+    relay(2)
     gather.round(3)
-    relay(2)
+    relay(3)
     gather.round(4)
-    relay(3)
+    relay(4)
+    relay(5)
     gather.round(5)
-    relay(4)
-
+    gather.round(6)
     @pl.loop(0, width // tile)
     def _(i):
         c = cols(i, tile)
         gz[0:length, c] = gz[0:length, c] + dot(zall[z, 0:length, :], gram[z, :, c])
         gz[length:, c] = dot(zall[z, length:, :], gram[z, :, c])
 
-    relay(5)
+    relay(6)
     add(0, 4, up, down)
-    relay(6)
-    for i in range(4):
-        distant(i)
+    relay(7)
+    add(4, 4, up, down)
+    distant(0, 4)
     add(0, 4, far)
-    add(4, 2, up, down)
-    relay(7)
-    distant(4)
-    distant(5)
+    distant(4, 2)
     add(4, 2, far)
-    add(6, 2, up, down)
-    distant(6)
-    distant(7)
+    distant(6, 2)
     add(6, 2, far)
 
     def norm_back(h, target, i):
@@ -473,23 +480,27 @@
         o, ot = o_buf[:, c], ot_buf[:, c]
         gzh, gzt = gz[0:length, c], gz[length:, c]
         r = lax.rsqrt(jnp.mean(o * o, axis=1, keepdims=True) + EPS)
-        m = jnp.mean(o * ot, axis=1, keepdims=True)
-        m1 = jnp.mean(o * gzh, axis=1, keepdims=True)
-        m1t = jnp.mean(ot * gzh + o * gzt, axis=1, keepdims=True)
-        r3 = r * r * r
-        g = r * gzh - (r3 * m1) * o
-        gt = r * gzt - (r3 * m) * gzh - (r3 * m1) * ot + (3.0 * r3 * r * r * m * m1 - r3 * m1t) * o
-        g_buf[:, c] = g.astype(BF16)
-        gt_buf[:, c] = gt.astype(BF16)
+        r2 = r * r
+        r3 = r2 * r
+        mean = jnp.mean(o * ot, axis=1, keepdims=True)
+        m = r3 * mean
+        m1 = r3 * jnp.mean(o * gzh, axis=1, keepdims=True)
+        m1t = r3 * jnp.mean(ot * gzh + o * gzt, axis=1, keepdims=True)
+        g = r * gzh - m1 * o
+        gt = r * gzt - m * gzh - m1 * ot + (3.0 * r2 * mean * m1 - m1t) * o
+        for value, top, rest in ((g, g_buf, g_rest), (gt, gt_buf, gt_rest)):
+            high = value.astype(BF16)
+            top[:, c] = high
+            rest[:, c] = (value - high.astype(F32)).astype(BF16)
         gd = (dq * g).astype(BF16)
         gtd = (dq * gt).astype(BF16)
         both = dot(q[:, c], jnp.concatenate([gd, gtd], axis=1), ((0,), (0,)))
         target[i, 0] = both[:, :d].astype(BF16)
         target[i, 1] = (both[:, d:] + dot(qt[:, c], gd, ((0,), (0,)))).astype(BF16)
 
-    pl.loop(0, heads // 2)(lambda i: norm_back(backward.theirs(i), backward.gift, i))
+    pl.loop(0, heads // 2, unroll=UNROLL)(lambda i: norm_back(backward.theirs(i), backward.gift, i))
     backward.give()
-    pl.loop(0, heads // 2)(lambda i: norm_back(backward.mine(i), backward.own, i))
+    pl.loop(0, heads // 2, unroll=UNROLL)(lambda i: norm_back(backward.mine(i), backward.own, i))
     arrival(backward.peer, backward.pair_sem.at[1])
     backward.combine()
     backward.out()
@@ -503,8 +514,12 @@
         at = dot(jnp.concatenate([qth, qh], axis=1), jnp.concatenate([kh, kth], axis=1), ((1,), (1,)))
         p = (a * w).astype(BF16)
         pt = (at * w).astype(BF16)
-        b = (dot(g, vh, ((1,), (1,))) * w).astype(BF16)
-        bt = dot(jnp.concatenate([gt, g], axis=1), jnp.concatenate([vh, vth], axis=1), ((1,), (1,)))
+        g_lo, gt_lo = g_rest[:, c], gt_rest[:, c]
+        b = dot(jnp.concatenate([g, g_lo], axis=1), jnp.concatenate([vh, vh], axis=1), ((1,), (1,)))
+        b = (b * w).astype(BF16)
+        bt = dot(
+            jnp.concatenate([gt, gt_lo, g, g_lo], axis=1), jnp.concatenate([vh, vh, vth, vth], axis=1), ((1,), (1,))
+        )
         bt = (bt * w).astype(BF16)
         s, st = forward.state[h, 0], forward.state[h, 1]
         outer = dot(jnp.concatenate([gt, g], axis=1), jnp.concatenate([s, st], axis=1), ((1,), (1,)))
@@ -512,13 +527,25 @@
             dot(jnp.concatenate([bt, b], axis=1), jnp.concatenate([kh, kth], axis=0)) + dq * outer
         ).astype(BF16)
         hk_buf[:, c] = dot(jnp.concatenate([bt, b], axis=0), jnp.concatenate([qh, qth], axis=0), ((0,), (0,)))
-        hv_buf[:, c] = dot(jnp.concatenate([pt, p], axis=0), jnp.concatenate([g, gt], axis=0), ((0,), (0,)))
+        hv_buf[:, c] = dot(
+            jnp.concatenate([pt, p, pt, p], axis=0), jnp.concatenate([g, gt, g_lo, gt_lo], axis=0), ((0,), (0,))
+        )
 
     pl.loop(0, heads // 2)(inner_back)
+    forward.finish()
+    forward.gift_copy.wait_send()
+    backward.gift_copy.wait_send()
+    gather.finish()
+
+    pltpu.make_async_copy(count.at[0:n - 1], count.at[0:n - 1], cs.at[0]).wait()
+    pltpu.make_async_copy(picked.at[0:3], picked.at[0:3], ws.at[0]).wait()
+    pltpu.make_async_copy(zall.at[0:3], zall.at[0:3], zs.at[0]).wait()
+
     backward.out_wait()
     backward.scan()
     backward.home()
     pl.loop(heads // 2, heads)(inner_back)
+    pltpu.make_async_copy(hq, results[0], out_sem.at[0]).start()
     backward.home_wait()
     backward.settle()
 
@@ -532,26 +559,22 @@
         hk[:, c] = (hk_buf[:, c] + w * ks).astype(BF16)
         hv[:, c] = (hv_buf[:, c] + w * vs).astype(BF16)
 
-    pl.loop(0, heads // 2)(last)
-    backward.settle_wait()
-    pl.loop(heads // 2, heads)(last)
-    forward.finish()
+    def emit(kind, h):
+        c = cols(h, d)
+        pltpu.make_async_copy((hk, hv)[kind].at[:, c], results[1 + kind].at[:, c], out_sem.at[1 + kind]).start()
+
+    for i in range(heads):
+        if i >= heads // 2:
+            backward.settle_wait(i - heads // 2)
+        last(i)
+        if i:
+            emit(0, lax.rem(backward.mine(i - 1), heads))
+            emit(1, lax.rem(backward.mine(i - 1), heads))
+    emit(0, lax.rem(backward.mine(heads - 1), heads))
+    emit(1, lax.rem(backward.mine(heads - 1), heads))
     backward.finish()
-    for copy in w_copies:
-        copy.wait_send()
-    gather.finish()
-
-    @pl.loop(1, n)
-    def _(step):
-        j = lax.rem(me + step, n)
-        remote(mine.at[0], count.at[me], cs.at[j], cr.at[me], seq=j).wait_send()
-
-    @pl.loop(0, heads)
-    def _(i):
-        c = cols(i, d)
-        whole, top = zall.at[z, :, c], zall.at[z, 0:length, c]
-        for kind, piece in enumerate((whole, whole, top, top)):
-            remote(piece, piece, zs.at[i, kind], zr.at[i, kind], head=up).wait_send()
+    for kind, buffer in enumerate((hq, hk, hv)):
+        pltpu.make_async_copy(buffer, results[kind], out_sem.at[kind]).wait()
 
 
 def store_kernel(*refs):
@@ -567,7 +590,7 @@
     heads = table.shape[0]
     d = width // heads
     flags = flags.reshape(1, length)
-    vmem, smem, hbm = (pl.BlockSpec(memory_space=m) for m in (pltpu.VMEM, pltpu.SMEM, pltpu.HBM))
+    vmem, hbm = (pl.BlockSpec(memory_space=m) for m in (pltpu.VMEM, pltpu.HBM))
     pair = pltpu.VMEM((heads // 2, 2, d, d), BF16)
     slots = pltpu.VMEM((n // 2, 2 * heads * d // n, d), BF16)
     scan = [pair, pair, pair, slots, slots, slots, slots, pltpu.VMEM((heads, 2, d, d), BF16), pair]
@@ -578,8 +601,8 @@
     results = pl.pallas_call(
         functools.partial(kernel, n, heads, groups),
         out_shape=(out, out, out),
-        in_specs=[hbm] * 6 + [smem, vmem] + [hbm] * 2,
-        out_specs=[vmem] * 3,
+        in_specs=[hbm] * 10,
+        out_specs=[pl.BlockSpec(memory_space=pl.ANY)] * 3,
         scratch_shapes=[
             *[narrow] * 6, pltpu.VMEM(weight.shape, BF16), pltpu.VMEM(goal.shape, BF16),
             pltpu.VMEM((length, length), F32), pltpu.VMEM((length, length), F32),
@@ -591,12 +614,14 @@
             pltpu.VMEM((groups, 2 * length, width), BF16),
             pltpu.VMEM((2 * length, width), F32),
             wide, wide, narrow, narrow, wide, wide,
-            *([dma((4,))] + [dma((n // 2,))] * 4) * 2,
-            dma((9,)), dma((n,)), dma((n,)), dma((4,)), dma((4,)), dma((36,)), dma((n, 2)), dma((heads, 4)), dma((heads, 4)),
+            *[dma((3 + heads // 2,)), dma((4,))] * 2,
+            dma((11,)), dma((1,)), dma((2,)), dma((1,)), dma((3,)), dma((1,)), dma((13,)), dma((1,)), dma((2 * heads + 3,)),
+            narrow, narrow, narrow, narrow, narrow, pltpu.SMEM(table.shape, jnp.int32), pltpu.VMEM(flags.shape, jnp.int32),
+            dma((3,)),
         ],
         compiler_params=pltpu.CompilerParams(collective_id=0, has_side_effects=True, vmem_limit_bytes=52 << 20),
         name="retention_hvp",
-    )(probe, source, content, probe_t, source_t, content_t, table, flags, weight, goal)
+    )(probe, source, content, probe_t, source_t, content_t, *(pltpu.with_memory_space_constraint(x, pltpu.HBM) for x in (table, flags)), weight, goal)
     return pl.pallas_call(
         store_kernel,
         out_shape=(out, out, out),

time: 93.1 us -> 81.6 us (0.88)
  Pallas kernels: 91 us -> 80.9 us
  local copies, waits for them, and re-layouts: 1.33 us -> 0 us
    pallas_call x1, Pallas kernels: 89.8 us -> 79.7 us  [on_device(): pl.pallas_call(functools.partial(kernel, n, heads, groups), out_shape=(ou...]
    unnamed x4 -> x0, local copies, waits for them, and re-layouts: 1.33 us -> none
where the time goes in v3:
time: 81.6 us; the launch traced here: 81.5 us
  Pallas kernels  80.9 us (99%)
    pallas_call x1, Pallas kernels, on_device(): pl.pallas_call(functools.partial(kernel, n, heads, groups), out_shape=(ou...  79.7 us

profile of v3, /device:TPU:1, one launch (start us, length us, event | category | flops | bytes accessed | tf_op | source)
XLA Modules:
  0.0 81.5 jit_solution(11326654570743411833)
XLA Ops:
  0.6 79.7 %retention_hvp.1 = (bf16[256,1024]{1,0:T(8,128)(2,1)S(1)}, bf16[256,1024]{1,0:T(8,128)(2,1)S(1)}, bf16[256,1024]{1,0:T(8,128)(2,1)S(1)}) custom-call(bf16[256,1024]{1,0:T(8,128)(2,1)} %refs_0_.1, bf16[256,1024]{1,0:T(8,128)(2,1)} %refs_1_.1, bf16[256,1024]{1,0:T(8,128)(2,1)} %refs_2_.1, bf16[256,1024]{1,0:T(8,128)(2,1)} %refs_3_.1, ...), custom_call_target="tpu_custom_call" | custom-call | tf_op jit(solution)/shard_map/retention_hvp/pallas_call | solution.py:601
  80.4 1.2 %store.1 = (bf16[256,1024]{1,0:T(8,128)(2,1)}, bf16[256,1024]{1,0:T(8,128)(2,1)}, bf16[256,1024]{1,0:T(8,128)(2,1)}) custom-call(bf16[256,1024]{1,0:T(8,128)(2,1)S(1)} %get-tuple-element.6.refs_0_, bf16[256,1024]{1,0:T(8,128)(2,1)S(1)} %get-tuple-element.7.refs_1_, bf16[256,1024]{1,0:T(8,128)(2,1)S(1)} %get-tuple-element.8.refs_2_), custom_call_target="tpu_custom_call" | custom-call | tf_op jit(solution)/shard_map/store/pallas_call | solution.py:625

commit v4 on v3

--- a/solution.py
+++ b/solution.py
@@ -69,11 +69,13 @@
 
 
 class GramGather:
-    def __init__(self, me, full, send_sem, recv_sem):
+    def __init__(self, me, full, part, parts, send_sem, recv_sem):
         c = lax.rem(me, 2)
         x, y = lax.rem(me // 2, 4), me // 8
         self.me, self.c, self.f, self.s = me, c, x + c * (y - x), y + c * (x - y)
-        self.full, self.send_sem, self.recv_sem = full, send_sem, recv_sem
+        columns = full.shape[2] // parts
+        self.full = full.at[:, :, part * columns:(part + 1) * columns]
+        self.send_sem, self.recv_sem, self.base = send_sem.at[part], recv_sem, 13 * part
         self.rows = full.shape[1] // 32
 
     def at(self, df, s_off, absolute=False):
@@ -89,10 +91,10 @@
 
     def send(self, piece, to, lane, half=None):
         view = self.view(piece, half)
-        remote(view, view, self.send_sem.at[0], self.recv_sem.at[lane], seq=to).start()
+        remote(view, view, self.send_sem, self.recv_sem.at[self.base + lane], seq=to).start()
 
     def wait(self, piece, lane):
-        arrival(self.view(piece), self.recv_sem.at[lane])
+        arrival(self.view(piece), self.recv_sem.at[self.base + lane])
 
     def spread(self, piece, df):
         self.send(piece, self.at(0, 1), self.lane(-1, df))
@@ -136,27 +138,29 @@
                 self.pass_on(step, 2, half)
         elif k == 5:
             four = self.full.at[:, 0:4 * self.rows, :]
-            arrival(four, self.recv_sem.at[11])
+            arrival(four, self.recv_sem.at[self.base + 11])
             for df in range(4):
                 self.sideways(self.at(df, 2))
         else:
-            arrival(self.full.at[:, 0:16 * self.rows, :], self.recv_sem.at[12])
+            arrival(self.full.at[:, 0:16 * self.rows, :], self.recv_sem.at[self.base + 12])
 
     def finish(self):
         sent = self.full.at[:, 0:31 * self.rows, :]
-        pltpu.make_async_copy(sent, sent, self.send_sem.at[0]).wait()
+        pltpu.make_async_copy(sent, sent, self.send_sem).wait()
 
 
 class Scan:
+    PARTS = 2
+
     def __init__(self, me, n, heads, length, lg, count, buffers, sems, reverse):
         self.own, self.gift, self.peer, self.tot, self.recv, self.back, self.entry, self.state, self.gift2 = buffers
-        self.pair_sem, hop_sem = sems
-        self.s1, self.r1, self.s2, self.r2 = (hop_sem.at[i] for i in range(4))
+        self.pair_sem, self.hop_sem = sems
         self.c, self.chip, self.chips = lax.rem(me, 2), me // 2, n // 2
         self.sibling = me + 1 - 2 * self.c
         self.half = heads // 2
+        self.step = self.half // self.PARTS
         self.length, self.lg, self.count, self.reverse = length, lg, count, reverse
-        self.per = self.chips // self.half
+        self.per = self.chips // self.step
         self.rows = self.tot.shape[1] // 2
         self.d = self.tot.shape[2]
 
@@ -166,92 +170,102 @@
     def theirs(self, i):
         return self.half * (1 - self.c) + i
 
-    def give(self):
-        self.gift_copy = remote(self.gift, self.peer, self.pair_sem.at[0], self.pair_sem.at[1], seq=self.sibling)
-        self.gift_copy.start()
+    def members(self, part):
+        return range(part * self.step, (part + 1) * self.step)
+
+    def give(self, part):
+        some = slice(part * self.step, (part + 1) * self.step)
+        remote(
+            self.gift.at[some], self.peer.at[some], self.pair_sem.at[0], self.pair_sem.at[2 + part], seq=self.sibling
+        ).start()
+
+    def give_wait(self, part):
+        arrival(self.peer.at[part * self.step:(part + 1) * self.step], self.pair_sem.at[2 + part])
 
     def decay(self, h, core):
         return jnp.exp(float(self.length) * self.lg[h, :, 0:self.d] + KEPT_LOG * self.count[2 * self.chip + core])
 
-    def ordered(self, i, part):
-        mine, peer = self.own[i, part].astype(F32), self.peer[i, part].astype(F32)
+    def ordered(self, i, half):
+        mine, peer = self.own[i, half].astype(F32), self.peer[i, half].astype(F32)
         return jnp.where(self.c == 0, mine, peer), jnp.where(self.c == 0, peer, mine)
 
-    def combine(self):
-        @pl.loop(0, self.half)
-        def _(i):
+    def slices(self, i):
+        first = (i // self.step) * self.chips + (i % self.step) * self.per
+        return slice(first, first + self.per)
+
+    def combine(self, part):
+        for i in self.members(part):
             factor = self.decay(self.mine(i), 0 if self.reverse else 1)
-            for part in range(2):
-                first, second = self.ordered(i, part)
+            for half in range(2):
+                first, second = self.ordered(i, half)
                 total = first + factor * second if self.reverse else first * factor + second
-                self.tot[pl.ds(i * self.per, self.per), part * self.rows:(part + 1) * self.rows, :] = (
+                self.tot[self.slices(i), half * self.rows:(half + 1) * self.rows, :] = (
                     total.astype(BF16).reshape(self.per, self.rows, self.d)
                 )
 
-    def spread(self, src, dst, send_sem, recv_sem):
+    def spread(self, part, src, dst, hop):
+        base = part * self.chips
+        send_sem, recv_sem = self.hop_sem.at[4 * part + 2 * hop], self.hop_sem.at[4 * part + 2 * hop + 1]
+
         @pl.loop(1, self.chips)
         def _(step):
             p = lax.rem(self.chip + step, self.chips)
-            remote(src.at[p], dst.at[self.chip], send_sem, recv_sem, seq=2 * p + self.c).start()
-
-    def collect(self, src, dst, send_sem, recv_sem):
+            remote(src.at[base + p], dst.at[base + self.chip], send_sem, recv_sem, seq=2 * p + self.c).start()
+
+    def collect(self, part, src, dst, hop):
         sent, got = src.at[0:self.chips - 1], dst.at[0:self.chips - 1]
-        pltpu.make_async_copy(sent, sent, send_sem).wait()
-        arrival(got, recv_sem)
-
-    def out(self):
-        self.spread(self.tot, self.recv, self.s1, self.r1)
-
-    def out_wait(self):
-        self.collect(self.tot, self.recv, self.s1, self.r1)
-
-    def scan(self):
-        self.recv[self.chip] = self.tot[self.chip]
-        lg = self.lg[self.mine(self.chip // self.per), :, 0:self.d]
+        pltpu.make_async_copy(sent, sent, self.hop_sem.at[4 * part + 2 * hop]).wait()
+        arrival(got, self.hop_sem.at[4 * part + 2 * hop + 1])
+
+    def out(self, part):
+        self.spread(part, self.tot, self.recv, 0)
+
+    def out_wait(self, part):
+        self.collect(part, self.tot, self.recv, 0)
+
+    def scan(self, part):
+        base = part * self.chips
+        self.recv[base + self.chip] = self.tot[base + self.chip]
+        lg = self.lg[self.mine(part * self.step + self.chip // self.per), :, 0:self.d]
 
         def step(i, run):
             p = self.chips - 1 - i if self.reverse else i
-            self.back[p] = run.astype(BF16)
+            self.back[base + p] = run.astype(BF16)
             factor = jnp.exp(2.0 * self.length * lg + KEPT_LOG * (self.count[2 * p] + self.count[2 * p + 1]))
-            return run * factor + self.recv[p].astype(F32)
+            return run * factor + self.recv[base + p].astype(F32)
 
         lax.fori_loop(0, self.chips, step, jnp.zeros(self.recv.shape[1:], F32))
-        self.entry[self.chip] = self.back[self.chip]
-
-    def home(self):
-        self.spread(self.back, self.entry, self.s2, self.r2)
-
-    def home_wait(self):
-        self.collect(self.back, self.entry, self.s2, self.r2)
-
-    def settle(self):
-        @pl.loop(0, self.half)
-        def _(i):
+        self.entry[base + self.chip] = self.back[base + self.chip]
+
+    def home(self, part):
+        self.spread(part, self.back, self.entry, 1)
+
+    def home_wait(self, part):
+        self.collect(part, self.back, self.entry, 1)
+
+    def settle(self, part):
+        for i in self.members(part):
             factor = self.decay(self.mine(i), 1 if self.reverse else 0)
-            for part in range(2):
-                first, second = self.ordered(i, part)
-                edge = self.entry[pl.ds(i * self.per, self.per), part * self.rows:(part + 1) * self.rows, :]
+            for half in range(2):
+                first, second = self.ordered(i, half)
+                edge = self.entry[self.slices(i), half * self.rows:(half + 1) * self.rows, :]
                 edge = edge.reshape(self.d, self.d).astype(F32)
                 inside = factor * edge + (second if self.reverse else first)
                 keep = (self.c == 1) if self.reverse else (self.c == 0)
-                self.gift2[i, part] = jnp.where(keep, inside, edge).astype(BF16)
-                self.state[self.mine(i), part] = jnp.where(keep, edge, inside).astype(BF16)
-
-        self.gift2_copies = [
+                self.gift2[i, half] = jnp.where(keep, inside, edge).astype(BF16)
+                self.state[self.mine(i), half] = jnp.where(keep, edge, inside).astype(BF16)
+        for i in self.members(part):
             remote(
                 self.gift2.at[i], self.state.at[self.mine(i)],
-                self.pair_sem.at[2], self.pair_sem.at[3 + i], seq=self.sibling,
-            )
-            for i in range(self.half)
-        ]
-        for copy in self.gift2_copies:
-            copy.start()
+                self.pair_sem.at[1], self.pair_sem.at[4 + i], seq=self.sibling,
+            ).start()
 
     def settle_wait(self, i):
-        arrival(self.state.at[self.theirs(i)], self.pair_sem.at[3 + i])
+        arrival(self.state.at[self.theirs(i)], self.pair_sem.at[4 + i])
 
     def finish(self):
-        pltpu.make_async_copy(self.gift2, self.gift2, self.pair_sem.at[2]).wait()
+        pltpu.make_async_copy(self.gift, self.gift, self.pair_sem.at[0]).wait()
+        pltpu.make_async_copy(self.gift2, self.gift2, self.pair_sem.at[1]).wait()
 
 
 def kernel(n, heads, groups, *refs):
@@ -261,7 +275,7 @@
     (picked, gram, zall, gz, o_buf, ot_buf, g_buf, gt_buf, hk_buf, hv_buf) = refs[46:56]
     ahead_sems, behind_sems = refs[56:58], refs[58:60]
     (load_sem, cs, cr, ws, wr, gs, gr, zs, zr) = refs[60:69]
-    (hq, hk, hv, g_rest, gt_rest, table, flags, out_sem) = refs[69:]
+    (hq, hk, hv, g_rest, gt_rest, r_buf, rb_buf, q_turned, qt_turned, table, flags, out_sem) = refs[69:]
     me, z = lax.axis_index("seq"), lax.axis_index("head")
     up, down = lax.rem(z + 1, groups), lax.rem(z + groups - 1, groups)
     far = lax.rem(z + 2, groups)
@@ -317,15 +331,24 @@
     w_send(z, high, 1, down)
     w_send(z, high, 2, up)
     w_send(z, low, 2, down)
-    pl.loop(0, heads // 2, unroll=UNROLL)(lambda i: own_state(forward.theirs(i), forward.gift, i))
     remote(mine.at[0], count.at[me], cs.at[0], cr.at[0], seq=forward.sibling).start()
-    forward.give()
-
-    pl.loop(0, heads // 2, unroll=UNROLL)(lambda i: own_state(forward.mine(i), forward.own, i))
+
+    def own_part(part, whose, target):
+        pl.loop(2 * part, 2 * part + 2, unroll=2)(lambda i: own_state(whose(i), target, i))
+
+    own_part(0, forward.theirs, forward.gift)
+    forward.give(0)
+    own_part(0, forward.mine, forward.own)
+    own_part(1, forward.theirs, forward.gift)
+    forward.give(1)
     arrival(count.at[forward.sibling], cr.at[0])
-    arrival(forward.peer, forward.pair_sem.at[1])
-    forward.combine()
-    forward.out()
+    forward.give_wait(0)
+    forward.combine(0)
+    forward.out(0)
+    own_part(1, forward.mine, forward.own)
+    forward.give_wait(1)
+    forward.combine(1)
+    forward.out(1)
     loads[0].wait()
     loads[3].wait()
 
@@ -356,32 +379,33 @@
     arrival(picked.at[up, high], wr.at[1])
     w_send(up, high, 2, down)
     arrival(count.at[0:n - 2], cr.at[1])
-    forward.out_wait()
-    forward.scan()
-    forward.home()
+    forward.out_wait(0)
+    forward.scan(0)
+    forward.home(0)
+    forward.out_wait(1)
+    forward.scan(1)
+    forward.home(1)
     pl.loop(heads // 2, heads)(inner)
-    arrival(picked.at[0:2], wr.at[2])
-    loads[7].wait()
     tile = 256
 
-    @pl.loop(0, width // tile)
-    def _(i):
-        c = cols(i, tile)
+    def gram_tile(i):
+        c = slice(i * tile, (i + 1) * tile)
         part = dot(picked[...].reshape(groups * rows, weight.shape[1]), weight[c, :], ((1,), (1,)))
         gram[:, mine_rows, c] = part.astype(BF16).reshape(groups, rows, tile)
 
-    gather = GramGather(me, gram, gs, gr)
-    forward.home_wait()
-    forward.settle()
-    gather.round(0)
+    gathers = [GramGather(me, gram, part, 2, gs, gr) for part in range(2)]
+
+    def head_of(i):
+        part, place = i // 4, i % 4
+        return forward.mine(2 * part + place) if place < 2 else forward.theirs(2 * part + place - 2)
 
     def z_send(i):
-        c = cols(lax.rem(forward.mine(i), heads), d)
+        c = cols(head_of(i), d)
         remote(zall.at[z, :, c], zall.at[z, :, c], zs.at[0], zr.at[2 * i], head=up).start()
         remote(zall.at[z, :, c], zall.at[z, :, c], zs.at[0], zr.at[2 * i + 1], head=down).start()
 
     def output(i):
-        h = lax.rem(forward.mine(i), heads)
+        h = head_of(i)
         c = cols(h, d)
         dq = jnp.exp((pos[...] + 1.0) * lg[h, :, 0:d] + cum[...])
         s, st = forward.state[h, 0], forward.state[h, 1]
@@ -395,29 +419,41 @@
         zall[z, 0:length, c] = (o * r).astype(BF16)
         zall[z, length:, c] = (r * ot - o * (r * r * r * m)).astype(BF16)
 
-        if isinstance(i, int):
+        if i % 4:
             z_send(i - 1)
-        else:
-            pl.when(i > 0)(lambda: z_send(i - 1))
-
-    pl.loop(0, heads // 2)(output)
-    for i in range(heads // 2, heads):
-        forward.settle_wait(i - heads // 2)
-        output(i)
-    z_send(heads - 1)
+
+    forward.home_wait(0)
+    forward.settle(0)
+    output(0)
+    output(1)
+    for i in range(2):
+        forward.settle_wait(i)
+        output(2 + i)
+    z_send(3)
+    arrival(picked.at[0:2], wr.at[2])
+    loads[7].wait()
+    for part in range(2):
+        gram_tile(2 * part)
+        gram_tile(2 * part + 1)
+        gathers[part].round(0)
+    forward.home_wait(1)
+    forward.settle(1)
+    output(4)
+    output(5)
+    for i in range(2):
+        forward.settle_wait(2 + i)
+        output(6 + i)
+    z_send(7)
     loads[8].wait()
 
     def goal_tile(i):
         c = slice(i * tile, (i + 1) * tile)
         gz[0:length, c] = -dot(goal[...], weight[c, :], ((1,), (1,)))
 
-    def chunk(i):
-        return cols(lax.rem(forward.mine(i), heads), d)
-
     groups_of = (0, 0, 0, 0, 1, 1, 2, 2)
 
     def relay(i):
-        c = chunk(i)
+        c = cols(head_of(i), d)
         lane = 2 * heads + groups_of[i]
         arrival(zall.at[down, :, c], zr.at[2 * i])
         piece = zall.at[down, 0:length, c]
@@ -426,84 +462,106 @@
         piece = zall.at[up, length:, c]
         remote(piece, piece, zs.at[0], zr.at[lane], head=down).start()
 
-    def span(first, number):
-        return pl.ds(pl.multiple_of(lax.rem(forward.mine(first), heads) * d, number * d), number * d)
-
     def distant(first, number):
-        arrival(zall.at[far, :, span(first, number)], zr.at[2 * heads + groups_of[first]])
-
-    def add(first, number, *sources):
-        part = span(first, number)
-
-        @pl.loop(0, width // tile)
-        def _(i):
-            c = cols(i, tile)
+        arrival(zall.at[far, :, 0:number * d], zr.at[2 * heads + groups_of[first]])
+
+    def add(pairs, source):
+        parts = [pl.ds(pl.multiple_of(head_of(2 * p) * d, 2 * d), 2 * d) for p in pairs]
+
+        for i in range(width // tile):
+            c = slice(i * tile, (i + 1) * tile)
             for r in (slice(0, length), slice(length, 2 * length)):
-                gz[r, c] = sum((dot(zall[g, r, part], gram[g, part, c]) for g in sources), gz[r, c])
-
-    goal_tile(0)
-    goal_tile(1)
-    gather.round(1)
-    relay(0)
-    goal_tile(2)
-    relay(1)
-    gather.round(2)
-    goal_tile(3)
-    relay(2)
-    gather.round(3)
-    relay(3)
-    gather.round(4)
-    relay(4)
-    relay(5)
-    gather.round(5)
-    gather.round(6)
-    @pl.loop(0, width // tile)
-    def _(i):
-        c = cols(i, tile)
-        gz[0:length, c] = gz[0:length, c] + dot(zall[z, 0:length, :], gram[z, :, c])
-        gz[length:, c] = dot(zall[z, length:, :], gram[z, :, c])
-
-    relay(6)
-    add(0, 4, up, down)
-    relay(7)
-    add(4, 4, up, down)
-    distant(0, 4)
-    add(0, 4, far)
-    distant(4, 2)
-    add(4, 2, far)
-    distant(6, 2)
-    add(6, 2, far)
-
-    def norm_back(h, target, i):
+                gz[r, c] = sum((dot(zall[source, r, p], gram[source, p, c]) for p in parts), gz[r, c])
+
+    def add_whole(first, last, *sources, fresh=False):
+        for i in range(first, last):
+            c = slice(i * tile, (i + 1) * tile)
+            for r in (slice(0, length), slice(length, 2 * length)):
+                start = 0.0 if fresh and r.start else gz[r, c]
+                gz[r, c] = sum((dot(zall[g, r, :], gram[g, :, c]) for g in sources), start)
+
+    def prepare(h):
         c = cols(h, d)
         dq = jnp.exp((pos[...] + 1.0) * lg[h, :, 0:d] + cum[...])
         o, ot = o_buf[:, c], ot_buf[:, c]
+        r = lax.rsqrt(jnp.mean(o * o, axis=1, keepdims=True) + EPS)
+        m = r * r * jnp.mean(o * ot, axis=1, keepdims=True)
+        zf = o * r
+        o_buf[:, c] = zf
+        ot_buf[:, c] = r * ot - zf * m
+        r_buf[:, c] = jnp.broadcast_to(r, o.shape)
+        rb_buf[:, c] = jnp.broadcast_to(m, o.shape)
+        q_turned[c, :] = (q[:, c].astype(F32) * dq).T.astype(BF16)
+        qt_turned[c, :] = (qt[:, c].astype(F32) * dq).T.astype(BF16)
+
+    goal_tile(0)
+    gathers[0].round(1)
+    relay(0)
+    gathers[1].round(1)
+    goal_tile(1)
+    relay(1)
+    gathers[0].round(2)
+    goal_tile(2)
+    gathers[1].round(2)
+    relay(2)
+    gathers[0].round(3)
+    goal_tile(3)
+    gathers[1].round(3)
+    relay(3)
+    gathers[0].round(4)
+    relay(4)
+    pl.loop(0, 4)(prepare)
+    gathers[1].round(4)
+    relay(5)
+    gathers[0].round(5)
+    relay(6)
+    pl.loop(4, 8)(prepare)
+    gathers[1].round(5)
+    gathers[0].round(6)
+    add_whole(0, 2, z, fresh=True)
+    relay(7)
+    gathers[1].round(6)
+    add_whole(2, 4, z, fresh=True)
+    add_whole(0, 4, up, down)
+    distant(0, 4)
+    add((0, 1), far)
+    distant(4, 2)
+    add((2,), far)
+    distant(6, 2)
+    add((3,), far)
+
+    def norm_back(h, target, i):
+        c = cols(h, d)
+        zf, ztf = o_buf[:, c], ot_buf[:, c]
         gzh, gzt = gz[0:length, c], gz[length:, c]
-        r = lax.rsqrt(jnp.mean(o * o, axis=1, keepdims=True) + EPS)
-        r2 = r * r
-        r3 = r2 * r
-        mean = jnp.mean(o * ot, axis=1, keepdims=True)
-        m = r3 * mean
-        m1 = r3 * jnp.mean(o * gzh, axis=1, keepdims=True)
-        m1t = r3 * jnp.mean(ot * gzh + o * gzt, axis=1, keepdims=True)
-        g = r * gzh - m1 * o
-        gt = r * gzt - m * gzh - m1 * ot + (3.0 * r2 * mean * m1 - m1t) * o
+        a = jnp.mean(zf * gzh, axis=1, keepdims=True)
+        at = jnp.mean(ztf * gzh + zf * gzt, axis=1, keepdims=True)
+        r = r_buf[:, c]
+        g = r * (gzh - zf * a)
+        gt = r * (gzt - ztf * a - zf * at) - rb_buf[:, c] * g
         for value, top, rest in ((g, g_buf, g_rest), (gt, gt_buf, gt_rest)):
             high = value.astype(BF16)
             top[:, c] = high
             rest[:, c] = (value - high.astype(F32)).astype(BF16)
-        gd = (dq * g).astype(BF16)
-        gtd = (dq * gt).astype(BF16)
-        both = dot(q[:, c], jnp.concatenate([gd, gtd], axis=1), ((0,), (0,)))
+        both = dot(q_turned[c, :], jnp.concatenate([g, gt], axis=1).astype(BF16))
         target[i, 0] = both[:, :d].astype(BF16)
-        target[i, 1] = (both[:, d:] + dot(qt[:, c], gd, ((0,), (0,)))).astype(BF16)
-
-    pl.loop(0, heads // 2, unroll=UNROLL)(lambda i: norm_back(backward.theirs(i), backward.gift, i))
-    backward.give()
-    pl.loop(0, heads // 2, unroll=UNROLL)(lambda i: norm_back(backward.mine(i), backward.own, i))
-    arrival(backward.peer, backward.pair_sem.at[1])
-    backward.combine()
-    backward.out()
+        target[i, 1] = (both[:, d:] + dot(qt_turned[c, :], g.astype(BF16))).astype(BF16)
+
+    def norm_part(part, whose, target):
+        pl.loop(2 * part, 2 * part + 2, unroll=2)(lambda i: norm_back(whose(i), target, i))
+
+    norm_part(0, backward.theirs, backward.gift)
+    backward.give(0)
+    norm_part(0, backward.mine, backward.own)
+    backward.give_wait(0)
+    backward.combine(0)
+    backward.out(0)
+    norm_part(1, backward.theirs, backward.gift)
+    backward.give(1)
+    norm_part(1, backward.mine, backward.own)
+    backward.give_wait(1)
+    backward.combine(1)
+    backward.out(1)
 
     def inner_back(h):
         c = cols(h, d)
@@ -531,23 +589,24 @@
             jnp.concatenate([pt, p, pt, p], axis=0), jnp.concatenate([g, gt, g_lo, gt_lo], axis=0), ((0,), (0,))
         )
 
-    pl.loop(0, heads // 2)(inner_back)
+    pl.loop(0, 3)(inner_back)
     forward.finish()
-    forward.gift_copy.wait_send()
-    backward.gift_copy.wait_send()
-    gather.finish()
+    for gather in gathers:
+        gather.finish()
 
     pltpu.make_async_copy(count.at[0:n - 1], count.at[0:n - 1], cs.at[0]).wait()
     pltpu.make_async_copy(picked.at[0:3], picked.at[0:3], ws.at[0]).wait()
     pltpu.make_async_copy(zall.at[0:3], zall.at[0:3], zs.at[0]).wait()
 
-    backward.out_wait()
-    backward.scan()
-    backward.home()
-    pl.loop(heads // 2, heads)(inner_back)
+    backward.out_wait(0)
+    backward.scan(0)
+    backward.home(0)
+    pl.loop(3, 5)(inner_back)
+    backward.out_wait(1)
+    backward.scan(1)
+    backward.home(1)
+    pl.loop(5, heads)(inner_back)
     pltpu.make_async_copy(hq, results[0], out_sem.at[0]).start()
-    backward.home_wait()
-    backward.settle()
 
     def last(i):
         h = lax.rem(backward.mine(i), heads)
@@ -563,13 +622,23 @@
         c = cols(h, d)
         pltpu.make_async_copy((hk, hv)[kind].at[:, c], results[1 + kind].at[:, c], out_sem.at[1 + kind]).start()
 
-    for i in range(heads):
-        if i >= heads // 2:
-            backward.settle_wait(i - heads // 2)
+    def finish(i):
         last(i)
         if i:
             emit(0, lax.rem(backward.mine(i - 1), heads))
             emit(1, lax.rem(backward.mine(i - 1), heads))
+
+    backward.home_wait(0)
+    backward.settle(0)
+    finish(0)
+    finish(1)
+    backward.home_wait(1)
+    backward.settle(1)
+    finish(2)
+    finish(3)
+    for i in range(heads // 2):
+        backward.settle_wait(i)
+        finish(heads // 2 + i)
     emit(0, lax.rem(backward.mine(heads - 1), heads))
     emit(1, lax.rem(backward.mine(heads - 1), heads))
     backward.finish()
@@ -592,7 +661,7 @@
     flags = flags.reshape(1, length)
     vmem, hbm = (pl.BlockSpec(memory_space=m) for m in (pltpu.VMEM, pltpu.HBM))
     pair = pltpu.VMEM((heads // 2, 2, d, d), BF16)
-    slots = pltpu.VMEM((n // 2, 2 * heads * d // n, d), BF16)
+    slots = pltpu.VMEM((n // 2 * Scan.PARTS, 2 * heads * d // n // Scan.PARTS, d), BF16)
     scan = [pair, pair, pair, slots, slots, slots, slots, pltpu.VMEM((heads, 2, d, d), BF16), pair]
     narrow, wide = pltpu.VMEM((length, width), BF16), pltpu.VMEM((length, width), F32)
     rows = width // n
@@ -614,9 +683,10 @@
             pltpu.VMEM((groups, 2 * length, width), BF16),
             pltpu.VMEM((2 * length, width), F32),
             wide, wide, narrow, narrow, wide, wide,
-            *[dma((3 + heads // 2,)), dma((4,))] * 2,
-            dma((11,)), dma((1,)), dma((2,)), dma((1,)), dma((3,)), dma((1,)), dma((13,)), dma((1,)), dma((2 * heads + 3,)),
-            narrow, narrow, narrow, narrow, narrow, pltpu.SMEM(table.shape, jnp.int32), pltpu.VMEM(flags.shape, jnp.int32),
+            *[dma((4 + heads // 2,)), dma((4 * Scan.PARTS,))] * 2,
+            dma((11,)), dma((1,)), dma((2,)), dma((1,)), dma((3,)), dma((2,)), dma((26,)), dma((1,)), dma((2 * heads + 3,)),
+            narrow, narrow, narrow, narrow, narrow, wide, wide,
+            pltpu.VMEM((width, length), BF16), pltpu.VMEM((width, length), BF16), pltpu.SMEM(table.shape, jnp.int32), pltpu.VMEM(flags.shape, jnp.int32),
             dma((3,)),
         ],
         compiler_params=pltpu.CompilerParams(collective_id=0, has_side_effects=True, vmem_limit_bytes=52 << 20),

time: 81.6 us -> 78.9 us (0.967)
  Pallas kernels: 80.9 us -> 78 us
    pallas_call x1, Pallas kernels: 79.7 us -> 76.8 us  [on_device(): pl.pallas_call(functools.partial(kernel, n, heads, groups), out_shape=(ou...]
where the time goes in v4:
time: 78.9 us; the launch traced here: 78.8 us
  Pallas kernels  78 us (99%)
  between operations  0.8 us (1%)
    pallas_call x1, Pallas kernels, on_device(): pl.pallas_call(functools.partial(kernel, n, heads, groups), out_shape=(ou...  76.8 us

profile of v4, /device:TPU:1, one launch (start us, length us, event | category | flops | bytes accessed | tf_op | source)
XLA Modules:
  0.0 78.8 jit_solution(1236857059004059303)
XLA Ops:
  0.6 76.8 %retention_hvp.1 = (bf16[256,1024]{1,0:T(8,128)(2,1)S(1)}, bf16[256,1024]{1,0:T(8,128)(2,1)S(1)}, bf16[256,1024]{1,0:T(8,128)(2,1)S(1)}) custom-call(bf16[256,1024]{1,0:T(8,128)(2,1)} %refs_0_.1, bf16[256,1024]{1,0:T(8,128)(2,1)} %refs_1_.1, bf16[256,1024]{1,0:T(8,128)(2,1)} %refs_2_.1, bf16[256,1024]{1,0:T(8,128)(2,1)} %refs_3_.1, ...), custom_call_target="tpu_custom_call" | custom-call | tf_op jit(solution)/shard_map/retention_hvp/pallas_call | solution.py:670
  77.5 1.2 %store.1 = (bf16[256,1024]{1,0:T(8,128)(2,1)}, bf16[256,1024]{1,0:T(8,128)(2,1)}, bf16[256,1024]{1,0:T(8,128)(2,1)}) custom-call(bf16[256,1024]{1,0:T(8,128)(2,1)S(1)} %get-tuple-element.6.refs_0_, bf16[256,1024]{1,0:T(8,128)(2,1)S(1)} %get-tuple-element.7.refs_1_, bf16[256,1024]{1,0:T(8,128)(2,1)S(1)} %get-tuple-element.8.refs_2_), custom_call_target="tpu_custom_call" | custom-call | tf_op jit(solution)/shard_map/store/pallas_call | solution.py:695

commit v5 on v4

--- a/solution.py
+++ b/solution.py
@@ -26,7 +26,17 @@
     return pl.ds(pl.multiple_of(h * d, d), d)
 
 
-def decay_tables(flags_ref, dist, fall, pos, cum):
+def reset_counts(flags_ref, pos, cum):
+    t = pos.shape[0]
+    row = lax.broadcasted_iota(jnp.int32, (t, t), 0)
+    col = lax.broadcasted_iota(jnp.int32, (t, t), 1)
+    flags = jnp.broadcast_to(flags_ref[...].astype(F32), (t, t))
+    cum_col = jnp.sum(jnp.where(col <= row, flags, 0.0), axis=1, keepdims=True)
+    pos[...] = lax.broadcasted_iota(jnp.int32, pos.shape, 0).astype(F32)
+    cum[...] = KEPT_LOG * jnp.broadcast_to(cum_col, cum.shape)
+
+
+def decay_tables(flags_ref, dist, fall):
     t = dist.shape[0]
     row = lax.broadcasted_iota(jnp.int32, (t, t), 0)
     col = lax.broadcasted_iota(jnp.int32, (t, t), 1)
@@ -36,8 +46,6 @@
     cum_row = jnp.sum(jnp.where(row <= col, flag_col, 0.0), axis=0, keepdims=True)
     dist[...] = jnp.where(row >= col, (row - col).astype(F32), FAR)
     fall[...] = KEPT_LOG * (cum_col - cum_row)
-    pos[...] = lax.broadcasted_iota(jnp.int32, pos.shape, 0).astype(F32)
-    cum[...] = KEPT_LOG * jnp.broadcast_to(cum_col, cum.shape)
 
 
 def barrier_start(n, me, up, down):
@@ -207,9 +215,11 @@
         base = part * self.chips
         send_sem, recv_sem = self.hop_sem.at[4 * part + 2 * hop], self.hop_sem.at[4 * part + 2 * hop + 1]
 
-        @pl.loop(1, self.chips)
-        def _(step):
-            p = lax.rem(self.chip + step, self.chips)
+        x, y = lax.rem(self.chip, 4), self.chip // 4
+        for dy, dx in sorted(
+            ((a, b) for a in range(4) for b in range(4) if a or b), key=lambda t: -min(t[0], 4 - t[0]) - min(t[1], 4 - t[1])
+        ):
+            p = lax.rem(y + dy, 4) * 4 + lax.rem(x + dx, 4)
             remote(src.at[base + p], dst.at[base + self.chip], send_sem, recv_sem, seq=2 * p + self.c).start()
 
     def collect(self, part, src, dst, hop):
@@ -270,7 +280,9 @@
 
 def kernel(n, heads, groups, *refs):
     inputs, (table_hbm, flags_hbm, w_hbm, goal_hbm), results = refs[:6], refs[6:10], refs[10:13]
-    (q, k, v, qt, kt, vt, weight, goal, dist, fall, pos, cum, lg, mine, count) = refs[13:28]
+    (q, qt, both_kv, weight, goal, dist, fall, pos, cum, lg, mine, count) = refs[13:25]
+    k, v, kt, vt = (both_kv.at[i] for i in range(4))
+    refs = (None,) * 3 + refs
     ahead, behind = refs[28:37], refs[37:46]
     (picked, gram, zall, gz, o_buf, ot_buf, g_buf, gt_buf, hk_buf, hv_buf) = refs[46:56]
     ahead_sems, behind_sems = refs[56:58], refs[58:60]
@@ -284,16 +296,26 @@
     scale = d ** -0.5
     rows = width // n
     mine_rows = pl.ds(pl.multiple_of(me * rows, rows), rows)
-    sources = (*inputs, w_hbm.at[mine_rows], w_hbm, goal_hbm, table_hbm, flags_hbm)
+    core = lax.rem(me, 2)
+    mine_columns = pl.ds(pl.multiple_of(core * (width // 2), width // 2), width // 2)
+    their_columns = pl.ds(pl.multiple_of((1 - core) * (width // 2), width // 2), width // 2)
+    sources = (table_hbm, flags_hbm, w_hbm.at[mine_rows], inputs[0], inputs[3], w_hbm, goal_hbm)
     loads = [
         pltpu.make_async_copy(src, dst, load_sem.at[i])
-        for i, (src, dst) in enumerate(zip(sources, (q, k, v, qt, kt, vt, picked.at[z], weight, goal, table, flags)))
+        for i, (src, dst) in enumerate(zip(sources, (table, flags, picked.at[z], q, qt, weight, goal)))
     ]
-    for i in (9, 10, 6, 1, 2, 4, 5, 0, 3, 7, 8):
-        loads[i].start()
+    loads[0].start()
+    loads[1].start()
+    for sem, columns in ((7, their_columns), (8, mine_columns)):
+        for i, j in enumerate((1, 2, 4, 5)):
+            pltpu.make_async_copy(inputs[j].at[:, columns], both_kv.at[i, :, columns], load_sem.at[sem]).start()
+        if sem == 7:
+            loads[2].start()
+    for load in loads[3:]:
+        load.start()
     barrier_start(n, me, up, down)
-    loads[9].wait()
-    loads[10].wait()
+    loads[0].wait()
+    loads[1].wait()
 
     @pl.loop(0, heads)
     def _(h):
@@ -301,14 +323,13 @@
         rates = jnp.exp(math.log(1.0 / 32.0) + fraction * math.log(16.0 / (length * n)))
         lg[h] = jnp.log1p(-rates)
 
-    decay_tables(flags, dist, fall, pos, cum)
+    reset_counts(flags, pos, cum)
     total = jnp.broadcast_to(jnp.sum(flags[...].astype(F32), axis=1, keepdims=True), (1, 128))
     mine[0] = total
     count[me] = total
     forward = Scan(me, n, heads, length, lg, count, ahead, ahead_sems, False)
     backward = Scan(me, n, heads, length, lg, count, behind, behind_sems, True)
-    for i in (1, 2, 4, 5):
-        loads[i].wait()
+    arrival(both_kv.at[:, :, their_columns], load_sem.at[7])
 
     def own_state(h, target, i):
         c = cols(h, d)
@@ -319,7 +340,12 @@
         target[i, 0] = both[:, :d].astype(BF16)
         target[i, 1] = (both[:, d:] + dot(ktw, v[:, c], ((0,), (0,)))).astype(BF16)
 
-    loads[6].wait()
+    def own_part(part, whose, target):
+        pl.loop(2 * part, 2 * part + 2, unroll=2)(lambda i: own_state(whose(i), target, i))
+
+    own_part(0, forward.theirs, forward.gift)
+    own_part(1, forward.theirs, forward.gift)
+    loads[2].wait()
     barrier_end(n)
     half = rows // 2
     low, high = slice(0, half), slice(half, rows)
@@ -333,14 +359,10 @@
     w_send(z, low, 2, down)
     remote(mine.at[0], count.at[me], cs.at[0], cr.at[0], seq=forward.sibling).start()
 
-    def own_part(part, whose, target):
-        pl.loop(2 * part, 2 * part + 2, unroll=2)(lambda i: own_state(whose(i), target, i))
-
-    own_part(0, forward.theirs, forward.gift)
     forward.give(0)
+    forward.give(1)
+    arrival(both_kv.at[:, :, mine_columns], load_sem.at[8])
     own_part(0, forward.mine, forward.own)
-    own_part(1, forward.theirs, forward.gift)
-    forward.give(1)
     arrival(count.at[forward.sibling], cr.at[0])
     forward.give_wait(0)
     forward.combine(0)
@@ -349,8 +371,8 @@
     forward.give_wait(1)
     forward.combine(1)
     forward.out(1)
-    loads[0].wait()
     loads[3].wait()
+    loads[4].wait()
 
     def inner(h):
         c = cols(h, d)
@@ -373,6 +395,7 @@
         def _():
             remote(mine.at[0], count.at[me], cs.at[0], cr.at[1], seq=j).start()
 
+    decay_tables(flags, dist, fall)
     pl.loop(0, heads // 2)(inner)
     arrival(picked.at[down, low], wr.at[0])
     w_send(down, low, 2, up)
@@ -401,8 +424,8 @@
 
     def z_send(i):
         c = cols(head_of(i), d)
-        remote(zall.at[z, :, c], zall.at[z, :, c], zs.at[0], zr.at[2 * i], head=up).start()
-        remote(zall.at[z, :, c], zall.at[z, :, c], zs.at[0], zr.at[2 * i + 1], head=down).start()
+        remote(zall.at[z, :, c], zall.at[z, :, c], zs.at[0], zr.at[i], head=up).start()
+        remote(zall.at[z, :, c], zall.at[z, :, c], zs.at[0], zr.at[i], head=down).start()
 
     def output(i):
         h = head_of(i)
@@ -419,8 +442,7 @@
         zall[z, 0:length, c] = (o * r).astype(BF16)
         zall[z, length:, c] = (r * ot - o * (r * r * r * m)).astype(BF16)
 
-        if i % 4:
-            z_send(i - 1)
+        z_send(i)
 
     forward.home_wait(0)
     forward.settle(0)
@@ -429,9 +451,8 @@
     for i in range(2):
         forward.settle_wait(i)
         output(2 + i)
-    z_send(3)
     arrival(picked.at[0:2], wr.at[2])
-    loads[7].wait()
+    loads[5].wait()
     for part in range(2):
         gram_tile(2 * part)
         gram_tile(2 * part + 1)
@@ -443,8 +464,7 @@
     for i in range(2):
         forward.settle_wait(2 + i)
         output(6 + i)
-    z_send(7)
-    loads[8].wait()
+    loads[6].wait()
 
     def goal_tile(i):
         c = slice(i * tile, (i + 1) * tile)
@@ -452,18 +472,33 @@
 
     groups_of = (0, 0, 0, 0, 1, 1, 2, 2)
 
-    def relay(i):
+    def near(i):
+        arrival(zall.at[0:2, :, cols(head_of(i), d)], zr.at[i])
+
+    def forward_on(i):
         c = cols(head_of(i), d)
-        lane = 2 * heads + groups_of[i]
-        arrival(zall.at[down, :, c], zr.at[2 * i])
+        lane = heads + groups_of[i]
         piece = zall.at[down, 0:length, c]
         remote(piece, piece, zs.at[0], zr.at[lane], head=up).start()
-        arrival(zall.at[up, :, c], zr.at[2 * i + 1])
         piece = zall.at[up, length:, c]
         remote(piece, piece, zs.at[0], zr.at[lane], head=down).start()
 
+    def relay(i):
+        near(i)
+        forward_on(i)
+
+    def relay_early(i):
+        near(i)
+        pl.when(core == 0)(lambda: forward_on(i))
+
+    def forward_late():
+        @pl.when(core == 1)
+        def _():
+            forward_on(6)
+            forward_on(7)
+
     def distant(first, number):
-        arrival(zall.at[far, :, 0:number * d], zr.at[2 * heads + groups_of[first]])
+        arrival(zall.at[far, :, 0:number * d], zr.at[heads + groups_of[first]])
 
     def add(pairs, source):
         parts = [pl.ds(pl.multiple_of(head_of(2 * p) * d, 2 * d), 2 * d) for p in pairs]
@@ -514,15 +549,17 @@
     gathers[1].round(4)
     relay(5)
     gathers[0].round(5)
-    relay(6)
+    relay_early(6)
     pl.loop(4, 8)(prepare)
     gathers[1].round(5)
     gathers[0].round(6)
     add_whole(0, 2, z, fresh=True)
-    relay(7)
+    relay_early(7)
     gathers[1].round(6)
     add_whole(2, 4, z, fresh=True)
-    add_whole(0, 4, up, down)
+    add_whole(0, 2, up, down)
+    forward_late()
+    add_whole(2, 4, up, down)
     distant(0, 4)
     add((0, 1), far)
     distant(4, 2)
@@ -552,12 +589,12 @@
 
     norm_part(0, backward.theirs, backward.gift)
     backward.give(0)
+    norm_part(1, backward.theirs, backward.gift)
+    backward.give(1)
     norm_part(0, backward.mine, backward.own)
     backward.give_wait(0)
     backward.combine(0)
     backward.out(0)
-    norm_part(1, backward.theirs, backward.gift)
-    backward.give(1)
     norm_part(1, backward.mine, backward.own)
     backward.give_wait(1)
     backward.combine(1)
@@ -589,7 +626,7 @@
             jnp.concatenate([pt, p, pt, p], axis=0), jnp.concatenate([g, gt, g_lo, gt_lo], axis=0), ((0,), (0,))
         )
 
-    pl.loop(0, 3)(inner_back)
+    pl.loop(0, 4)(inner_back)
     forward.finish()
     for gather in gathers:
         gather.finish()
@@ -601,11 +638,10 @@
     backward.out_wait(0)
     backward.scan(0)
     backward.home(0)
-    pl.loop(3, 5)(inner_back)
     backward.out_wait(1)
     backward.scan(1)
     backward.home(1)
-    pl.loop(5, heads)(inner_back)
+    pl.loop(4, heads)(inner_back)
     pltpu.make_async_copy(hq, results[0], out_sem.at[0]).start()
 
     def last(i):
@@ -624,9 +660,8 @@
 
     def finish(i):
         last(i)
-        if i:
-            emit(0, lax.rem(backward.mine(i - 1), heads))
-            emit(1, lax.rem(backward.mine(i - 1), heads))
+        emit(0, lax.rem(backward.mine(i), heads))
+        emit(1, lax.rem(backward.mine(i), heads))
 
     backward.home_wait(0)
     backward.settle(0)
@@ -639,8 +674,6 @@
     for i in range(heads // 2):
         backward.settle_wait(i)
         finish(heads // 2 + i)
-    emit(0, lax.rem(backward.mine(heads - 1), heads))
-    emit(1, lax.rem(backward.mine(heads - 1), heads))
     backward.finish()
     for kind, buffer in enumerate((hq, hk, hv)):
         pltpu.make_async_copy(buffer, results[kind], out_sem.at[kind]).wait()
@@ -673,7 +706,7 @@
         in_specs=[hbm] * 10,
         out_specs=[pl.BlockSpec(memory_space=pl.ANY)] * 3,
         scratch_shapes=[
-            *[narrow] * 6, pltpu.VMEM(weight.shape, BF16), pltpu.VMEM(goal.shape, BF16),
+            narrow, narrow, pltpu.VMEM((4, length, width), BF16), pltpu.VMEM(weight.shape, BF16), pltpu.VMEM(goal.shape, BF16),
             pltpu.VMEM((length, length), F32), pltpu.VMEM((length, length), F32),
             pltpu.VMEM((length, d), F32), pltpu.VMEM((length, d), F32),
             pltpu.VMEM((heads, 1, length), F32), pltpu.VMEM((1, 1, d), F32), pltpu.VMEM((n, 1, d), F32),
@@ -684,7 +717,7 @@
             pltpu.VMEM((2 * length, width), F32),
             wide, wide, narrow, narrow, wide, wide,
             *[dma((4 + heads // 2,)), dma((4 * Scan.PARTS,))] * 2,
-            dma((11,)), dma((1,)), dma((2,)), dma((1,)), dma((3,)), dma((2,)), dma((26,)), dma((1,)), dma((2 * heads + 3,)),
+            dma((9,)), dma((1,)), dma((2,)), dma((1,)), dma((3,)), dma((2,)), dma((26,)), dma((1,)), dma((heads + 3,)),
             narrow, narrow, narrow, narrow, narrow, wide, wide,
             pltpu.VMEM((width, length), BF16), pltpu.VMEM((width, length), BF16), pltpu.SMEM(table.shape, jnp.int32), pltpu.VMEM(flags.shape, jnp.int32),
             dma((3,)),

time: 78.9 us -> 76.3 us (0.967)
  Pallas kernels: 78 us -> 75.3 us
    pallas_call x1, Pallas kernels: 76.8 us -> 74.2 us  [on_device(): pl.pallas_call(functools.partial(kernel, n, heads, groups), out_shape=(ou...]
where the time goes in v5:
time: 76.3 us; the launch traced here: 76.1 us
  Pallas kernels  75.3 us (99%)
  between operations  0.8 us (1%)
    pallas_call x1, Pallas kernels, on_device(): pl.pallas_call(functools.partial(kernel, n, heads, groups), out_shape=(ou...  74.2 us

profile of v5, /device:TPU:1, one launch (start us, length us, event | category | flops | bytes accessed | tf_op | source)
XLA Modules:
  0.0 76.1 jit_solution(12566856812774617740)
XLA Ops:
  0.6 74.2 %retention_hvp.1 = (bf16[256,1024]{1,0:T(8,128)(2,1)S(1)}, bf16[256,1024]{1,0:T(8,128)(2,1)S(1)}, bf16[256,1024]{1,0:T(8,128)(2,1)S(1)}) custom-call(bf16[256,1024]{1,0:T(8,128)(2,1)} %refs_0_.1, bf16[256,1024]{1,0:T(8,128)(2,1)} %refs_1_.1, bf16[256,1024]{1,0:T(8,128)(2,1)} %refs_2_.1, bf16[256,1024]{1,0:T(8,128)(2,1)} %refs_3_.1, ...), custom_call_target="tpu_custom_call" | custom-call | tf_op jit(solution)/shard_map/retention_hvp/pallas_call | solution.py:703
  74.8 1.2 %store.1 = (bf16[256,1024]{1,0:T(8,128)(2,1)}, bf16[256,1024]{1,0:T(8,128)(2,1)}, bf16[256,1024]{1,0:T(8,128)(2,1)}) custom-call(bf16[256,1024]{1,0:T(8,128)(2,1)S(1)} %get-tuple-element.6.refs_0_, bf16[256,1024]{1,0:T(8,128)(2,1)S(1)} %get-tuple-element.7.refs_1_, bf16[256,1024]{1,0:T(8,128)(2,1)S(1)} %get-tuple-element.8.refs_2_), custom_call_target="tpu_custom_call" | custom-call | tf_op jit(solution)/shard_map/store/pallas_call | solution.py:728

commit v6 on v5

--- a/solution.py
+++ b/solution.py
@@ -160,14 +160,14 @@
 class Scan:
     PARTS = 2
 
-    def __init__(self, me, n, heads, length, lg, count, buffers, sems, reverse):
+    def __init__(self, me, n, heads, length, lg, count, totals, buffers, sems, reverse):
         self.own, self.gift, self.peer, self.tot, self.recv, self.back, self.entry, self.state, self.gift2 = buffers
         self.pair_sem, self.hop_sem = sems
         self.c, self.chip, self.chips = lax.rem(me, 2), me // 2, n // 2
         self.sibling = me + 1 - 2 * self.c
         self.half = heads // 2
         self.step = self.half // self.PARTS
-        self.length, self.lg, self.count, self.reverse = length, lg, count, reverse
+        self.length, self.lg, self.count, self.totals, self.reverse = length, lg, count, totals, reverse
         self.per = self.chips // self.step
         self.rows = self.tot.shape[1] // 2
         self.d = self.tot.shape[2]
@@ -191,7 +191,7 @@
         arrival(self.peer.at[part * self.step:(part + 1) * self.step], self.pair_sem.at[2 + part])
 
     def decay(self, h, core):
-        return jnp.exp(float(self.length) * self.lg[h, :, 0:self.d] + KEPT_LOG * self.count[2 * self.chip + core])
+        return jnp.exp(float(self.length) * self.lg[h, :, 0:self.d] + KEPT_LOG * self.count[core])
 
     def ordered(self, i, half):
         mine, peer = self.own[i, half].astype(F32), self.peer[i, half].astype(F32)
@@ -211,15 +211,17 @@
                     total.astype(BF16).reshape(self.per, self.rows, self.d)
                 )
 
-    def spread(self, part, src, dst, hop):
-        base = part * self.chips
-        send_sem, recv_sem = self.hop_sem.at[4 * part + 2 * hop], self.hop_sem.at[4 * part + 2 * hop + 1]
-
+    def others(self):
         x, y = lax.rem(self.chip, 4), self.chip // 4
         for dy, dx in sorted(
             ((a, b) for a in range(4) for b in range(4) if a or b), key=lambda t: -min(t[0], 4 - t[0]) - min(t[1], 4 - t[1])
         ):
-            p = lax.rem(y + dy, 4) * 4 + lax.rem(x + dx, 4)
+            yield lax.rem(y + dy, 4) * 4 + lax.rem(x + dx, 4)
+
+    def spread(self, part, src, dst, hop):
+        base = part * self.chips
+        send_sem, recv_sem = self.hop_sem.at[4 * part + 2 * hop], self.hop_sem.at[4 * part + 2 * hop + 1]
+        for p in self.others():
             remote(src.at[base + p], dst.at[base + self.chip], send_sem, recv_sem, seq=2 * p + self.c).start()
 
     def collect(self, part, src, dst, hop):
@@ -241,10 +243,10 @@
         def step(i, run):
             p = self.chips - 1 - i if self.reverse else i
             self.back[base + p] = run.astype(BF16)
-            factor = jnp.exp(2.0 * self.length * lg + KEPT_LOG * (self.count[2 * p] + self.count[2 * p + 1]))
+            factor = jnp.exp(2.0 * self.length * lg + KEPT_LOG * self.totals[p])
             return run * factor + self.recv[base + p].astype(F32)
 
-        lax.fori_loop(0, self.chips, step, jnp.zeros(self.recv.shape[1:], F32))
+        lax.fori_loop(0, self.chips, step, jnp.zeros(self.recv.shape[1:], F32), unroll=self.chips)
         self.entry[base + self.chip] = self.back[base + self.chip]
 
     def home(self, part):
@@ -280,9 +282,9 @@
 
 def kernel(n, heads, groups, *refs):
     inputs, (table_hbm, flags_hbm, w_hbm, goal_hbm), results = refs[:6], refs[6:10], refs[10:13]
-    (q, qt, both_kv, weight, goal, dist, fall, pos, cum, lg, mine, count) = refs[13:25]
+    (q, qt, both_kv, weight, goal, dist, fall, pos, cum, lg, mine, count, totals) = refs[13:26]
     k, v, kt, vt = (both_kv.at[i] for i in range(4))
-    refs = (None,) * 3 + refs
+    refs = (None,) * 2 + refs
     ahead, behind = refs[28:37], refs[37:46]
     (picked, gram, zall, gz, o_buf, ot_buf, g_buf, gt_buf, hk_buf, hv_buf) = refs[46:56]
     ahead_sems, behind_sems = refs[56:58], refs[58:60]
@@ -326,9 +328,9 @@
     reset_counts(flags, pos, cum)
     total = jnp.broadcast_to(jnp.sum(flags[...].astype(F32), axis=1, keepdims=True), (1, 128))
     mine[0] = total
-    count[me] = total
-    forward = Scan(me, n, heads, length, lg, count, ahead, ahead_sems, False)
-    backward = Scan(me, n, heads, length, lg, count, behind, behind_sems, True)
+    count[core] = total
+    forward = Scan(me, n, heads, length, lg, count, totals, ahead, ahead_sems, False)
+    backward = Scan(me, n, heads, length, lg, count, totals, behind, behind_sems, True)
     arrival(both_kv.at[:, :, their_columns], load_sem.at[7])
 
     def own_state(h, target, i):
@@ -357,15 +359,18 @@
     w_send(z, high, 1, down)
     w_send(z, high, 2, up)
     w_send(z, low, 2, down)
-    remote(mine.at[0], count.at[me], cs.at[0], cr.at[0], seq=forward.sibling).start()
+    remote(mine.at[0], count.at[core], cs.at[0], cr.at[0], seq=forward.sibling).start()
 
     forward.give(0)
     forward.give(1)
     arrival(both_kv.at[:, :, mine_columns], load_sem.at[8])
     own_part(0, forward.mine, forward.own)
-    arrival(count.at[forward.sibling], cr.at[0])
+    arrival(count.at[1 - core], cr.at[0])
+    totals[forward.chip] = count[0] + count[1]
     forward.give_wait(0)
     forward.combine(0)
+    for p in forward.others():
+        remote(totals.at[forward.chip], totals.at[forward.chip], cs.at[0], cr.at[1], seq=2 * p + core).start()
     forward.out(0)
     own_part(1, forward.mine, forward.own)
     forward.give_wait(1)
@@ -387,28 +392,20 @@
         o_buf[:, c] = both[:, :d]
         ot_buf[:, c] = both[:, d:] + dot(pt, v[:, c])
 
-    @pl.loop(1, n)
-    def _(step):
-        j = lax.rem(me + step, n)
-
-        @pl.when(j != forward.sibling)
-        def _():
-            remote(mine.at[0], count.at[me], cs.at[0], cr.at[1], seq=j).start()
-
     decay_tables(flags, dist, fall)
-    pl.loop(0, heads // 2)(inner)
+    pl.loop(0, heads // 2, unroll=2)(inner)
     arrival(picked.at[down, low], wr.at[0])
     w_send(down, low, 2, up)
     arrival(picked.at[up, high], wr.at[1])
     w_send(up, high, 2, down)
-    arrival(count.at[0:n - 2], cr.at[1])
+    arrival(totals.at[0:n // 2 - 1], cr.at[1])
     forward.out_wait(0)
     forward.scan(0)
     forward.home(0)
     forward.out_wait(1)
     forward.scan(1)
     forward.home(1)
-    pl.loop(heads // 2, heads)(inner)
+    pl.loop(heads // 2, heads, unroll=2)(inner)
     tile = 256
 
     def gram_tile(i):
@@ -626,12 +623,12 @@
             jnp.concatenate([pt, p, pt, p], axis=0), jnp.concatenate([g, gt, g_lo, gt_lo], axis=0), ((0,), (0,))
         )
 
-    pl.loop(0, 4)(inner_back)
+    pl.loop(0, 4, unroll=2)(inner_back)
     forward.finish()
     for gather in gathers:
         gather.finish()
 
-    pltpu.make_async_copy(count.at[0:n - 1], count.at[0:n - 1], cs.at[0]).wait()
+    pltpu.make_async_copy(totals, totals, cs.at[0]).wait()
     pltpu.make_async_copy(picked.at[0:3], picked.at[0:3], ws.at[0]).wait()
     pltpu.make_async_copy(zall.at[0:3], zall.at[0:3], zs.at[0]).wait()
 
@@ -641,7 +638,7 @@
     backward.out_wait(1)
     backward.scan(1)
     backward.home(1)
-    pl.loop(4, heads)(inner_back)
+    pl.loop(4, heads, unroll=2)(inner_back)
     pltpu.make_async_copy(hq, results[0], out_sem.at[0]).start()
 
     def last(i):
@@ -709,7 +706,7 @@
             narrow, narrow, pltpu.VMEM((4, length, width), BF16), pltpu.VMEM(weight.shape, BF16), pltpu.VMEM(goal.shape, BF16),
             pltpu.VMEM((length, length), F32), pltpu.VMEM((length, length), F32),
             pltpu.VMEM((length, d), F32), pltpu.VMEM((length, d), F32),
-            pltpu.VMEM((heads, 1, length), F32), pltpu.VMEM((1, 1, d), F32), pltpu.VMEM((n, 1, d), F32),
+            pltpu.VMEM((heads, 1, length), F32), pltpu.VMEM((1, 1, d), F32), pltpu.VMEM((2, 1, d), F32), pltpu.VMEM((n // 2, 1, d), F32),
             *scan, *scan,
             pltpu.VMEM((groups, rows, weight.shape[1]), BF16),
             pltpu.VMEM((groups, width, width), BF16),

time: 76.3 us -> 74.2 us (0.972)
  Pallas kernels: 75.3 us -> 73.3 us
    pallas_call x1, Pallas kernels: 74.2 us -> 72.2 us  [on_device(): pl.pallas_call(functools.partial(kernel, n, heads, groups), out_shape=(ou...]
where the time goes in v6:
time: 74.2 us; the launch traced here: 74.1 us
  Pallas kernels  73.3 us (99%)
  between operations  0.8 us (1%)
    pallas_call x1, Pallas kernels, on_device(): pl.pallas_call(functools.partial(kernel, n, heads, groups), out_shape=(ou...  72.2 us

profile of v6, /device:TPU:1, one launch (start us, length us, event | category | flops | bytes accessed | tf_op | source)
XLA Modules:
  0.0 74.1 jit_solution(16755426251701106512)
XLA Ops:
  0.6 72.2 %retention_hvp.1 = (bf16[256,1024]{1,0:T(8,128)(2,1)S(1)}, bf16[256,1024]{1,0:T(8,128)(2,1)S(1)}, bf16[256,1024]{1,0:T(8,128)(2,1)S(1)}) custom-call(bf16[256,1024]{1,0:T(8,128)(2,1)} %refs_0_.1, bf16[256,1024]{1,0:T(8,128)(2,1)} %refs_1_.1, bf16[256,1024]{1,0:T(8,128)(2,1)} %refs_2_.1, bf16[256,1024]{1,0:T(8,128)(2,1)} %refs_3_.1, ...), custom_call_target="tpu_custom_call" | custom-call | tf_op jit(solution)/shard_map/retention_hvp/pallas_call | solution.py:700
  72.8 1.2 %store.1 = (bf16[256,1024]{1,0:T(8,128)(2,1)}, bf16[256,1024]{1,0:T(8,128)(2,1)}, bf16[256,1024]{1,0:T(8,128)(2,1)}) custom-call(bf16[256,1024]{1,0:T(8,128)(2,1)S(1)} %get-tuple-element.6.refs_0_, bf16[256,1024]{1,0:T(8,128)(2,1)S(1)} %get-tuple-element.7.refs_1_, bf16[256,1024]{1,0:T(8,128)(2,1)S(1)} %get-tuple-element.8.refs_2_), custom_call_target="tpu_custom_call" | custom-call | tf_op jit(solution)/shard_map/store/pallas_call | solution.py:725

commit v7 on v6

--- a/solution.py
+++ b/solution.py
@@ -445,15 +445,17 @@
     forward.settle(0)
     output(0)
     output(1)
+    arrival(picked.at[0:2], wr.at[2])
+    loads[5].wait()
+    gram_tile(0)
+    gram_tile(1)
+    gathers[0].round(0)
     for i in range(2):
         forward.settle_wait(i)
         output(2 + i)
-    arrival(picked.at[0:2], wr.at[2])
-    loads[5].wait()
-    for part in range(2):
-        gram_tile(2 * part)
-        gram_tile(2 * part + 1)
-        gathers[part].round(0)
+    gram_tile(2)
+    gram_tile(3)
+    gathers[1].round(0)
     forward.home_wait(1)
     forward.settle(1)
     output(4)

time: 74.2 us -> 74.5 us (level)
  no operation moved by 1% of the time
where the time goes in v7:
time: 74.5 us; the launch traced here: 74.4 us
  Pallas kernels  73.6 us (99%)
  between operations  0.8 us (1%)
    pallas_call x1, Pallas kernels, on_device(): pl.pallas_call(functools.partial(kernel, n, heads, groups), out_shape=(ou...  72.4 us

profile of v7, /device:TPU:1, one launch (start us, length us, event | category | flops | bytes accessed | tf_op | source)
XLA Modules:
  0.0 74.4 jit_solution(8927504357454580399)
XLA Ops:
  0.6 72.4 %retention_hvp.1 = (bf16[256,1024]{1,0:T(8,128)(2,1)S(1)}, bf16[256,1024]{1,0:T(8,128)(2,1)S(1)}, bf16[256,1024]{1,0:T(8,128)(2,1)S(1)}) custom-call(bf16[256,1024]{1,0:T(8,128)(2,1)} %refs_0_.1, bf16[256,1024]{1,0:T(8,128)(2,1)} %refs_1_.1, bf16[256,1024]{1,0:T(8,128)(2,1)} %refs_2_.1, bf16[256,1024]{1,0:T(8,128)(2,1)} %refs_3_.1, ...), custom_call_target="tpu_custom_call" | custom-call | tf_op jit(solution)/shard_map/retention_hvp/pallas_call | solution.py:702
  73.0 1.2 %store.1 = (bf16[256,1024]{1,0:T(8,128)(2,1)}, bf16[256,1024]{1,0:T(8,128)(2,1)}, bf16[256,1024]{1,0:T(8,128)(2,1)}) custom-call(bf16[256,1024]{1,0:T(8,128)(2,1)S(1)} %get-tuple-element.6.refs_0_, bf16[256,1024]{1,0:T(8,128)(2,1)S(1)} %get-tuple-element.7.refs_1_, bf16[256,1024]{1,0:T(8,128)(2,1)S(1)} %get-tuple-element.8.refs_2_), custom_call_target="tpu_custom_call" | custom-call | tf_op jit(solution)/shard_map/store/pallas_call | solution.py:727
